TPU v7x, 8 devices: a whole 2x2x1 slice. The times are simulated.
8 devices in a mesh: dp: 2 (over z, y), ep: 4 (over x, core).
Axes of the slice: x: 2, y: 2, z: 1, core: 2. Of those that a mesh axis runs over, the one named last changes fastest.
Arguments:
- h0: bfloat16 [8, 128, 2048], P(('dp', 'ep')), parts along dimension 0
- idx: int32 [8, 128, 8], P(('dp', 'ep')), parts along dimension 0
- slot: int32 [8, 128, 8], P(('dp', 'ep')), parts along dimension 0
- norm_attn: bfloat16 [2048], replicated
- wq: bfloat16 [2048, 4096], replicated
- wk: bfloat16 [2048, 512], replicated
- wv: bfloat16 [2048, 512], replicated
- wo: bfloat16 [4096, 2048], replicated
- norm_ffn: bfloat16 [2048], replicated
- w1: bfloat16 [2048, 6144], replicated
- w3: bfloat16 [2048, 6144], replicated
- w2: bfloat16 [6144, 2048], replicated
- norm_moe: bfloat16 [2048], replicated
- wr: bfloat16 [2048, 128], replicated
- ue1: bfloat16 [128, 2048, 768], P('ep')
- ue3: bfloat16 [128, 2048, 768], P('ep')
- ue2: bfloat16 [128, 768, 2048], P('ep')
Outputs:
- output: bfloat16 [8, 128, 2048], P(('dp', 'ep')), parts along dimension 0
There are 2 independent parts. A program takes and returns all parts, laid end to end along the dimension named above; an argument that names none is the same for every part.
All inputs are finite; a program needn't handle non-finite values.
Results may differ from a plain program's by a relative error of at most 0.0127889.
Values are sent between devices in bfloat16 or wider.
A program may use at most 1.75 GiB of HBM per device.

v0:
```python
import jax
import jax.numpy as jnp
from jax import lax
from jax.sharding import PartitionSpec as P

HEAD = 128
EPS = 1e-6
ROPE_BASE = 10000.0


def _rms(x, w):
    xf = x.astype(jnp.float32)
    r = lax.rsqrt(jnp.mean(xf * xf, axis=-1, keepdims=True) + EPS)
    return (xf * r * w.astype(jnp.float32)).astype(jnp.bfloat16)


def _rope(x, cos, sin):
    h = HEAD // 2
    x1, x2 = x[..., :h], x[..., h:]
    return jnp.concatenate([x1 * cos - x2 * sin, x2 * cos + x1 * sin], axis=-1)


def _dense(h0, na, wq, wk, wv, wo, nf, w1, w3, w2):
    f32, bf = jnp.float32, jnp.bfloat16
    b, s, d = h0.shape
    nh = wq.shape[1] // HEAD
    nkvv = wk.shape[1] // HEAD
    pos = jnp.arange(s).astype(f32)
    inv = ROPE_BASE ** (-2.0 * jnp.arange(HEAD // 2).astype(f32) / HEAD)
    ang = pos[:, None] * inv[None, :]
    cos, sin = jnp.cos(ang)[:, None, :], jnp.sin(ang)[:, None, :]
    x = _rms(h0, na).reshape(b * s, d)
    q = _rope(jnp.dot(x, wq, preferred_element_type=f32).reshape(b, s, nh, HEAD), cos, sin).astype(bf)
    k = _rope(jnp.dot(x, wk, preferred_element_type=f32).reshape(b, s, nkvv, HEAD), cos, sin).astype(bf)
    v = jnp.dot(x, wv, preferred_element_type=f32).astype(bf).reshape(b, s, nkvv, HEAD)
    q = q.reshape(b, s, nkvv, nh // nkvv, HEAD)
    sc = jnp.einsum('bqgrd,bkgd->bgrqk', q, k, preferred_element_type=f32) * HEAD ** -0.5
    causal = jnp.arange(s)[:, None] >= jnp.arange(s)[None, :]
    sc = jnp.where(causal, sc, -jnp.inf)
    p = jax.nn.softmax(sc, axis=-1).astype(bf)
    o = jnp.einsum('bgrqk,bkgd->bqgrd', p, v, preferred_element_type=f32).astype(bf).reshape(b * s, nh * HEAD)
    a = (h0.reshape(b * s, d).astype(f32) + jnp.dot(o, wo, preferred_element_type=f32)).astype(bf)
    z = _rms(a, nf)
    hid = (jax.nn.silu(jnp.dot(z, w1, preferred_element_type=f32)) * jnp.dot(z, w3, preferred_element_type=f32)).astype(bf)
    return a.astype(f32) + jnp.dot(hid, w2, preferred_element_type=f32)


def _route(h0, nm, wr, idx):
    d = h0.shape[-1]
    k = idx.shape[-1]
    u = _rms(h0, nm).reshape(-1, d)
    logits = jnp.dot(u, wr, preferred_element_type=jnp.float32)
    g = jax.nn.softmax(jnp.take_along_axis(logits, idx.reshape(-1, k), axis=1), axis=-1)
    return u, g


def _experts(x, ue1, ue3, ue2):
    f32 = jnp.float32
    h1 = jnp.einsum('ecd,edf->ecf', x, ue1, preferred_element_type=f32)
    h3 = jnp.einsum('ecd,edf->ecf', x, ue3, preferred_element_type=f32)
    hid = (jax.nn.silu(h1) * h3).astype(jnp.bfloat16)
    return jnp.einsum('ecf,efd->ecd', hid, ue2, preferred_element_type=f32).astype(jnp.bfloat16)


def solution(mesh):
    G = mesh.shape['ep']

    def local(h0, idx, slot, na, wq, wk, wv, wo, nf, w1, w3, w2, nm, wr, ue1, ue3, ue2):
        f32 = jnp.float32
        b, s, d = h0.shape
        t = b * s
        k = idx.shape[-1]
        el = ue1.shape[0]
        e = el * G
        cap = 2 * t * k // e
        u, g = _route(h0, nm, wr, idx)
        ix = idx.reshape(t, k)
        sl = slot.reshape(t, k)
        rows = jnp.broadcast_to(jnp.arange(t, dtype=jnp.int32)[:, None], (t, k))
        tok = jnp.full((e, cap), t, jnp.int32).at[ix, sl].set(rows)
        send = jnp.take(u, tok, axis=0, mode='fill', fill_value=0)
        recv = lax.all_to_all(send, 'ep', 0, 0, tiled=True)
        x = recv.reshape(G, el, cap, d).transpose(1, 0, 2, 3).reshape(el, G * cap, d)
        y = _experts(x, ue1, ue3, ue2)
        y = y.reshape(el, G, cap, d).transpose(1, 0, 2, 3).reshape(e, cap, d)
        back = lax.all_to_all(y, 'ep', 0, 0, tiled=True)
        yg = back[ix, sl]
        m = jnp.sum(g[..., None] * yg.astype(f32), axis=1)
        dense = _dense(h0, na, wq, wk, wv, wo, nf, w1, w3, w2)
        return (dense + m).astype(jnp.bfloat16).reshape(b, s, d)

    rows_spec = P(('dp', 'ep'))
    in_specs = (rows_spec,) * 3 + (P(),) * 11 + (P('ep'),) * 3
    return jax.shard_map(local, mesh=mesh, in_specs=in_specs, out_specs=rows_spec, check_vma=False)
```

profile of v0, /device:TPU:0, one launch (start us, length us, event | category | flops | bytes accessed | tf_op | source)
XLA Modules:
  0.0 411.7 jit_solution(10241758178395588292)
XLA Ops:
  0.0 0.0 copy-start
  0.0 0.9 shift-left_or_fusion
  0.9 0.7 and_reduce_fusion
  1.6 0.7 multiply_reduce_fusion.1
  2.3 0.1 copy.50
  2.4 0.1 reshape.356
  2.5 0.1 reshape.358
  2.6 4.3 %scatter_custom_fusion = s32[2048]{0:T(1024)S(1)} fusion(s32[1024]{0:T(1024)S(1)} %reshape.356, s32[1024]{0:T(1024)S(1)} %reshape.358, s32[]{:T(128)} %constant.33.clone.1), kind=kCustom, calls=%fused_computation.78 | custom fusion | bytes 8196
  7.0 0.7 convert_element_type.133
  7.7 1.2 fusion.15
  8.9 0.1 copy.52
  9.0 0.1 reshape.338
  9.1 0.1 copy.51
  9.2 1.2 fusion.21
  10.5 11.0 %gather_fusion = bf16[2048,2048]{1,0:T(8,128)(2,1)} fusion(bf16[128,2048]{1,0:T(8,128)(2,1)S(1)} %fusion.21, s32[2048]{0:T(1024)S(1)} %broadcast_clamp_fusion), kind=kCustom, calls=%fused_computation | custom fusion | bytes 16785408 | tf_op jit(solution)/shard_map/jit(_take)/gather | solution.py:81
  21.5 7.3 %broadcast_select_fusion = bf16[128,16,2048]{2,1,0:T(8,128)(2,1)} fusion(bf16[128,16,2048]{2,1,0:T(8,128)(2,1)} %bitcast.125, pred[128,16]{1,0:T(8,128)(4,1)S(1)} %copy.51), kind=kLoop, calls=%fused_computation.6 | loop fusion | flops 4194304 | bytes 16779264 | tf_op jit(solution)/shard_map/jit(_take)/select_n | solution.py:81
  28.7 6.0 %all-to-all-start = ((bf16[128,16,2048]{2,1,0:T(8,128)(2,1)}), bf16[128,16,2048]{2,1,0:T(8,128)(2,1)}, u32[]{:S(2)}, u32[]{:S(2)}) async-start(bf16[128,16,2048]{2,1,0:T(8,128)(2,1)} %broadcast_select_fusion), calls=%async_computation | async-start | bytes 16777216 | tf_op jit(solution)/shard_map/all_to_all | solution.py:82
  34.7 0.0 copy-done.8
  34.7 0.7 copy.48
  35.4 0.1 copy.55
  35.5 0.7 reshape.344
  36.2 0.1 copy.49
  36.3 0.1 reshape.350
  36.4 0.0 copy-done.7
  36.4 0.3 fusion.47
  36.7 0.0 copy-start.9
  36.7 0.0 copy-start.3
  36.7 6.8 %gather_fusion.2 = f32[1024]{0:T(1024)S(1)} fusion(f32[128,128]{1,0:T(8,128)S(1)} %fusion.47, s32[1024]{0:T(1024)S(1)} %reshape.350), kind=kCustom, calls=%fused_computation.2 | custom fusion | bytes 16384 | tf_op jit(solution)/shard_map/jit(take_along_axis)/gather | solution.py:53
  43.5 0.1 reshape.353
  43.6 0.0 copy-done.9
  43.7 0.5 convolution_convert_fusion.2
  44.2 0.1 copy.59
  44.3 22.6 %copy.63 = bf16[4096,2048]{1,0:T(8,128)(2,1)} copy(bf16[4096,2048]{0,1:T(8,128)(2,1)} %bitcast.126) | data formatting | bytes 33554432 | tf_op jit(solution)/shard_map/dot_general | solution.py:33
  66.9 0.2 multiply_cosine_fusion
  67.1 61.5 %all-to-all-done = bf16[128,16,2048]{2,1,0:T(8,128)(2,1)} async-done(((bf16[128,16,2048]{2,1,0:T(8,128)(2,1)}), bf16[128,16,2048]{2,1,0:T(8,128)(2,1)}, u32[]{:S(2)}, u32[]{:S(2)}) %all-to-all-start) | async-done | bytes 8388640 | tf_op jit(solution)/shard_map/all_to_all | solution.py:82
  128.6 8.3 %copy.53 = bf16[32,4,16,2048]{3,2,1,0:T(8,128)(2,1)} copy(bf16[32,4,16,2048]{3,2,0,1:T(8,128)(2,1)} %bitcast.32) | data formatting | bytes 16777216 | tf_op jit(solution)/shard_map/transpose | solution.py:83
  136.8 38.1 %fusion.48 = f32[32,64,768]{2,1,0:T(8,128)} fusion(bf16[32,64,2048]{2,1,0:T(8,128)(2,1)} %bitcast.121, bf16[32,2048,768]{2,1,0:T(8,128)(2,1)} %param.31), kind=kOutput, calls=%fused_computation.91 | convolution fusion | flops 6442450944 | bytes 115343360 | tf_op jit(solution)/shard_map/ecd,edf->ecf/dot_general | solution.py:59
  174.9 38.8 %multiply_convert_fusion.8 = bf16[32,64,768]{2,1,0:T(8,128)(2,1)} fusion(f32[32,64,768]{2,1,0:T(8,128)} %fusion.48, bf16[32,64,2048]{2,1,0:T(8,128)(2,1)} %bitcast.122, bf16[32,2048,768]{2,1,0:T(8,128)(2,1)} %param.32), kind=kOutput, calls=%fused_computation.9.clone.clone.1 | convolution fusion | flops 6451888128 | bytes 118489088 | tf_op jit(solution)/shard_map/ecd,edf->ecf/dot_general | solution.py:60
  213.7 37.7 %convolution_convert_fusion = bf16[32,64,2048]{2,1,0:T(8,128)(2,1)} fusion(bf16[32,768,2048]{2,1,0:T(8,128)(2,1)} %param.33, bf16[32,64,768]{2,1,0:T(8,128)(2,1)} %multiply_convert_fusion.8), kind=kOutput, calls=%fused_computation.10 | convolution fusion | flops 6446645248 | bytes 112197632 | tf_op jit(solution)/shard_map/ecf,efd->ecd/dot_general | solution.py:62
  251.4 8.3 %copy.54 = bf16[4,32,16,2048]{3,2,1,0:T(8,128)(2,1)} copy(bf16[4,32,16,2048]{3,2,0,1:T(8,128)(2,1)} %bitcast.123) | data formatting | bytes 16777216 | tf_op jit(solution)/shard_map/transpose | solution.py:85
  259.7 5.9 %all-to-all-start.1 = ((bf16[128,16,2048]{2,1,0:T(8,128)(2,1)}), bf16[128,16,2048]{2,1,0:T(8,128)(2,1)}, u32[]{:S(2)}, u32[]{:S(2)}) async-start(bf16[128,16,2048]{2,1,0:T(8,128)(2,1)} %bitcast.124), calls=%async_computation.1 | async-start | bytes 16777216 | tf_op jit(solution)/shard_map/all_to_all | solution.py:86
  265.6 8.3 %convolution_bitcast_fusion = f32[1,128,32,128]{1,3,2,0:T(8,128)S(1)} fusion(bf16[32,128,2048]{2,1,0:T(8,128)(2,1)} %bitcast.120, bf16[1,128,2048]{2,1,0:T(8,128)(2,1)S(1)} %copy-done.3, f32[2048]{0:T(1024)S(1)} %convert_element_type.119, f32[128]{0:T(128)S(1)} %add_rsqrt_fusion.1), kind=kOutput, calls=%fused_computation.24 | convolution fusion | flops 2148532224 | bytes 19407360 | tf_op jit(solution)/shard_map/dot_general | solution.py:33
  273.8 0.0 copy-start.10
  273.9 0.0 copy-start.6
  273.9 1.1 subtract_convert_fusion
  275.0 2.4 copy.44
  277.3 1.4 copy.43
  278.7 2.9 copy.60
  281.7 0.0 copy-done.6
  281.7 0.1 fusion.42
  281.8 0.2 fusion.36
  282.0 0.8 convolution_bitcast_fusion.1
  282.9 2.5 fusion.46
  285.4 0.3 fusion.10
  285.7 0.6 convolution_convert_fusion.1
  286.3 8.2 %multiply_reduce_fusion = (f32[128]{0:T(128)S(1)}, f32[128,2048]{1,0:T(8,128)S(1)}) fusion(bf16[128,4096]{0,1:T(8,128)(2,1)S(1)} %bitcast.131, bf16[4096,2048]{1,0:T(8,128)(2,1)} %param.24, bf16[1,128,2048]{2,1,0:T(8,128)(2,1)S(1)} %copy-done.3), kind=kOutput, calls=%fused_computation.41 | convolution fusion | flops 2149056512 | bytes 19399168 | tf_op jit(solution)/shard_map/dot_general | solution.py:42
  294.5 0.1 fusion.35
  294.7 13.6 %fusion.20 = f32[128,6144]{1,0:T(8,128)} fusion(bf16[2048,6144]{1,0:T(8,128)(2,1)} %param.26, f32[128,2048]{1,0:T(8,128)S(1)} %get-tuple-element.18, f32[2048]{0:T(1024)S(1)} %convert_element_type.130, f32[128]{0:T(128)S(1)} %add_rsqrt_fusion), kind=kOutput, calls=%fused_computation.44 | convolution fusion | flops 3222011904 | bytes 29368832 | tf_op jit(solution)/shard_map/dot_general | solution.py:44
  308.3 0.0 copy-done.4
  308.3 49.9 %all-to-all-done.1 = bf16[128,16,2048]{2,1,0:T(8,128)(2,1)} async-done(((bf16[128,16,2048]{2,1,0:T(8,128)(2,1)}), bf16[128,16,2048]{2,1,0:T(8,128)(2,1)}, u32[]{:S(2)}, u32[]{:S(2)}) %all-to-all-start.1) | async-done | bytes 8388640 | tf_op jit(solution)/shard_map/all_to_all | solution.py:86
  358.2 0.0 copy-done.2
  358.2 25.5 %gather_fusion.1 = bf16[1024,2048]{1,0:T(8,128)(2,1)} fusion(bf16[128,16,2048]{2,1,0:T(8,128)(2,1)} %all-to-all-done.1, s32[1024]{0:T(1024)S(1)} %copy-done.2), kind=kCustom, calls=%fused_computation.1 | custom fusion | bytes 8396800 | tf_op jit(solution)/shard_map/gather | solution.py:87
  383.6 7.6 %fusion = f32[128,2048]{1,0:T(8,128)} fusion(bf16[1024,2048]{1,0:T(8,128)(2,1)} %gather_fusion.1, f32[128,8]{1,0:T(8,128)S(1)} %fusion.35), kind=kLoop, calls=%fused_computation.5 | loop fusion | flops 6029312 | bytes 5246976 | tf_op jit(solution)/shard_map/reduce_sum | solution.py:88
  391.2 20.5 %fusion.9 = bf16[1,128,2048]{2,1,0:T(8,128)(2,1)} fusion(f32[128,2048]{1,0:T(8,128)} %fusion, f32[128,2048]{1,0:T(8,128)S(1)} %copy-done.5, bf16[6144,2048]{1,0:T(8,128)(2,1)} %param.28, bf16[2048,6144]{1,0:T(8,128)(2,1)} %param.27, f32[128,6144]{1,0:T(8,128)} %fusion.20, f32[2048]{0:T(1024)S(1)} %convert_element_type.130, f32[128]{0:T(128)S(1)} %add_rsqrt_fusion), kind=kOutput, calls=%fused_computation.19 | convolution fusion | flops 6448742400 | bytes 56107520 | tf_op jit(solution)/shard_map/dot_general | solution.py:45
  (24 shorter events, 0.1 us)
Async XLA Ops:
  0.0 43.7 %copy-start = (bf16[2048,512]{1,0:T(8,128)(2,1)S(1)}, bf16[2048,512]{1,0:T(8,128)(2,1)}, u32[]{:S(2)}) copy-start(bf16[2048,512]{1,0:T(8,128)(2,1)} %param.23) | copy-start | bytes 6291460
  28.7 6.0 %copy-start.8 = (s32[1,128,8]{1,2,0:T(8,128)S(1)}, s32[1,128,8]{1,2,0:T(8,128)}, u32[]{:S(2)}) copy-start(s32[1,128,8]{1,2,0:T(8,128)} %param.18) | copy-start | bytes 12292
  28.7 7.7 %copy-start.7 = (bf16[2048,128]{1,0:T(8,128)(2,1)S(1)}, bf16[2048,128]{1,0:T(8,128)(2,1)}, u32[]{:S(2)}) copy-start(bf16[2048,128]{1,0:T(8,128)(2,1)} %param.30) | copy-start | bytes 1572868
  28.7 99.8 %all-to-all-start = ((bf16[128,16,2048]{2,1,0:T(8,128)(2,1)}), bf16[128,16,2048]{2,1,0:T(8,128)(2,1)}, u32[]{:S(2)}, u32[]{:S(2)}) async-start(bf16[128,16,2048]{2,1,0:T(8,128)(2,1)} %broadcast_select_fusion), calls=%async_computation | async-start | bytes 16777216 | tf_op jit(solution)/shard_map/all_to_all | solution.py:82
  36.7 6.9 %copy-start.9 = (bf16[2048]{0:T(1024)(128)(2,1)S(1)}, bf16[2048]{0:T(1024)(128)(2,1)}, u32[]{:S(2)}) copy-start(bf16[2048]{0:T(1024)(128)(2,1)} %param.20) | copy-start | bytes 12292
  36.7 6.9 %copy-start.3 = (bf16[1,128,2048]{2,1,0:T(8,128)(2,1)S(1)}, bf16[1,128,2048]{2,1,0:T(8,128)(2,1)}, u32[]{:S(2)}) copy-start(bf16[1,128,2048]{2,1,0:T(8,128)(2,1)} %param.17) | copy-start | bytes 1572868
  259.7 98.5 %all-to-all-start.1 = ((bf16[128,16,2048]{2,1,0:T(8,128)(2,1)}), bf16[128,16,2048]{2,1,0:T(8,128)(2,1)}, u32[]{:S(2)}, u32[]{:S(2)}) async-start(bf16[128,16,2048]{2,1,0:T(8,128)(2,1)} %bitcast.124), calls=%async_computation.1 | async-start | bytes 16777216 | tf_op jit(solution)/shard_map/all_to_all | solution.py:86
  273.8 7.8 %copy-start.10 = (bf16[2048]{0:T(1024)(128)(2,1)S(1)}, bf16[2048]{0:T(1024)(128)(2,1)}, u32[]{:S(2)}) copy-start(bf16[2048]{0:T(1024)(128)(2,1)} %param.25) | copy-start | bytes 12292
  273.9 7.9 %copy-start.6 = (s32[1,128,8]{2,1,0:T(8,128)S(1)}, s32[1,128,8]{2,1,0:T(8,128)}, u32[]{:S(2)}) copy-start(s32[1,128,8]{2,1,0:T(8,128)} %copy.48) | copy-start | bytes 12292
  294.5 13.8 %copy-start.4 = (f32[128,2048]{1,0:T(8,128)}, f32[128,2048]{1,0:T(8,128)S(1)}, u32[]{:S(2)}) copy-start(f32[128,2048]{1,0:T(8,128)S(1)} %get-tuple-element.18) | copy-start | bytes 3145732
  294.7 63.5 %copy-start.2 = (s32[1024]{0:T(1024)S(1)}, s32[1024]{0:T(1024)}, u32[]{:S(2)}) copy-start(s32[1024]{0:T(1024)} %reshape.344) | copy-start | bytes 12292
  358.2 33.0 %copy-start.5 = (f32[128,2048]{1,0:T(8,128)S(1)}, f32[128,2048]{1,0:T(8,128)}, u32[]{:S(2)}) copy-start(f32[128,2048]{1,0:T(8,128)} %copy-done.4) | copy-start | bytes 3145732
  391.2 20.5 %copy-start.1 = (bf16[2048,512]{1,0:T(8,128)(2,1)S(1)}, bf16[2048,512]{1,0:T(8,128)(2,1)}, u32[]{:S(2)}) copy-start(bf16[2048,512]{1,0:T(8,128)(2,1)} %param.23) | copy-start | bytes 6291460
where the time goes:
time: 413 us; the launch traced here: 412 us
  matrix products  170 us (41%)
  waiting for transfers between devices  111 us (27%)
  local copies, waits for them, and re-layouts  95.9 us (23%)
  other arithmetic  22.4 us (5%)
  starting transfers between devices  11.8 us (3%)
    all_to_all x1, waiting for transfers between devices, local(): recv = lax.all_to_all(send, 'ep', 0, 0, tiled=True)  61.5 us
    all_to_all x1, waiting for transfers between devices, local(): back = lax.all_to_all(y, 'ep', 0, 0, tiled=True)  49.9 us
    dot_general x1, matrix products, _experts(): h3 = jnp.einsum('ecd,edf->ecf', x, ue3, preferred_element_type=f32)  38.8 us
    dot_general x1, matrix products, _experts(): h1 = jnp.einsum('ecd,edf->ecf', x, ue1, preferred_element_type=f32)  38.1 us
    dot_general x1, matrix products, _experts(): jnp.einsum('ecf,efd->ecd', hid, ue2, preferred_element_type=f32)  37.7 us
    gather x1, local copies, waits for them, and re-layouts, local(): yg = back[ix, sl]  25.5 us
    dot_general x1, local copies, waits for them, and re-layouts, _dense(): jnp.dot(x, wq, preferred_element_type=f32).reshape(b, s, nh, HEAD)  22.6 us
    dot_general x1, matrix products, _dense(): return a.astype(f32) + jnp.dot(hid, w2, preferred_element_type=f32)  20.5 us
  transfers between devices with their start and end apart: 2, of which 2 were waited for; matrix products, arithmetic and copies ran while one was open for 18% of the time, Pallas kernels for 0%

commit v1 on v0

v1 whole, which is shorter than its diff:
```python
import functools

import jax
import jax.numpy as jnp
import numpy as np
from jax import lax
from jax.experimental import pallas as pl
from jax.experimental.pallas import tpu as pltpu
from jax.sharding import PartitionSpec as P

MESH = pl.DeviceIdType.MESH
HEAD = 128
EPS = 1e-6
ROPE_BASE = 10000.0

T, D, FE, FF, TOP, CAP = 128, 2048, 768, 6144, 8, 16
EL = 16
QT = 512
CW = 512
NC = D // CW
HW = CW // 2
NA = 4
NB = 4
NQ = 8
NF = FF // FE
N1 = 4
A_FF1 = 2 + NQ
A_EXP = A_FF1 + 2 * N1
A_FF2 = A_EXP + 2 * EL
A_END = A_FF2 + 2 * (NF - N1)
B_EXP = 8
B_W2 = B_EXP + 4 * NC
B_END = B_W2 + 8

f32, bf16 = jnp.float32, jnp.bfloat16


def _dot(a, b):
    return jnp.dot(a, b, preferred_element_type=f32)


def _kernel(h0, idx, slot, na, nf, nm, cos, sin, wr, wq, wk, wv, wo, w1, w3, w2, ue1, ue3, ue2, out,
            xz, ar, fs, u, info, ws, x, kk, vv, g, pp, rc, r1, r2, ra, rb,
            sem_a, sem_b, send, recv):
    dp, ep = lax.axis_index('dp'), lax.axis_index('ep')
    px = (dp, lax.rem(ep + 2, 4))
    py = (1 - dp, ep)
    pd = (1 - dp, lax.rem(ep + 2, 4))
    pc = (dp, ep + 1 - 2 * lax.rem(ep, 2))
    e0 = dp * EL

    def a_copy(kind, i, s):
        if kind == 'k':
            return pltpu.make_async_copy(wk, ra.at[s, :, pl.ds(0, QT)], sem_a.at[s])
        if kind == 'v':
            return pltpu.make_async_copy(wv, ra.at[s, :, pl.ds(0, QT)], sem_a.at[s])
        if kind == 'q':
            c = pl.multiple_of(i * QT, QT)
            return pltpu.make_async_copy(wq.at[:, pl.ds(c, QT)], ra.at[s, :, pl.ds(0, QT)], sem_a.at[s])
        if kind in ('w1', 'w3'):
            c = pl.multiple_of(i * FE, FE)
            return pltpu.make_async_copy((w1 if kind == 'w1' else w3).at[:, pl.ds(c, FE)], ra.at[s], sem_a.at[s])
        return pltpu.make_async_copy((ue1 if kind == 'e1' else ue3).at[e0 + i], ra.at[s], sem_a.at[s])

    def a_start(t, lo, hi):
        s = lax.rem(t, NA)

        def pairs(first, last, names, base):
            a, b = max(first, lo), min(last, hi)
            if a >= b:
                return
            for par in (0, 1):
                @pl.when((t >= a) & (t < b) & (lax.rem(t - first, 2) == par))
                def _():
                    a_copy(names[par], base + (t - first) // 2, s).start()

        if lo < A_FF1:
            @pl.when(t < A_FF1)
            def _():
                a_copy('q', t - 2, s).start()
        pairs(A_FF1, A_EXP, ('w1', 'w3'), 0)
        pairs(A_EXP, A_FF2, ('e1', 'e3'), 0)
        pairs(A_FF2, A_END, ('w1', 'w3'), N1)

    def b_copy(kind, i, s):
        if kind == 'wo':
            return pltpu.make_async_copy(
                wo.at[pl.ds(lax.rem(i, 2) * 4, 4), :, pl.ds(pl.multiple_of((i // 2) * CW, CW), CW)],
                rb.at[s, :, pl.ds(0, QT), :], sem_b.at[s])
        if kind == 'w2':
            return pltpu.make_async_copy(
                w2.at[pl.ds(lax.rem(i, 2) * 4, 4), :, pl.ds(pl.multiple_of((i // 2) * CW, CW), CW)],
                rb.at[s], sem_b.at[s])
        return pltpu.make_async_copy(
            ue2.at[pl.ds(e0 + lax.rem(i, 4) * 4, 4), :, pl.ds(pl.multiple_of((i // 4) * CW, CW), CW)],
            rb.at[s], sem_b.at[s])

    def b_start(t, lo, hi):
        s = lax.rem(t, NB)
        for first, last, name in ((0, B_EXP, 'wo'), (B_EXP, B_W2, 'e2'), (B_W2, B_END, 'w2')):
            a, b = max(first, lo), min(last, hi)
            if a >= b:
                continue

            @pl.when((t >= a) & (t < b))
            def _():
                b_copy(name, t - first, s).start()

    specs = {}

    def rdma(key, src, dst, to):
        i = specs.setdefault(key, len(specs))
        return pltpu.make_async_remote_copy(src_ref=src, dst_ref=dst, send_sem=send.at[i], recv_sem=recv.at[i],
                                            device_id=to, device_id_type=MESH)

    ag = {
        'ix': lambda: rdma('ix', info.at[0], info.at[2], px),
        'iy': lambda: rdma('iy', info.at[0], info.at[3], py),
        'id': lambda: rdma('id', info.at[0], info.at[6], pd),
        'ic': lambda: rdma('ic', info.at[0], info.at[1], pc),
        'x0': lambda: rdma('x0', u.at[0, 0], u.at[2, 0], px),
        'x1': lambda: rdma('x1', u.at[0, 1], u.at[2, 1], px),
        'y1': lambda: rdma('y1', u.at[0, 1], u.at[3, 1], py),
        'y0': lambda: rdma('y0', u.at[0, 0], u.at[3, 0], py),
        'c': lambda: rdma('c', u.at[0], u.at[1], pc),
        'd0': lambda: rdma('d0', u.at[2, 0], u.at[6, 0], py),
        'd1': lambda: rdma('d1', u.at[3, 1], u.at[6, 1], px),
        'cx': lambda: rdma('cx', u.at[2], u.at[4], pc),
        'cy': lambda: rdma('cy', u.at[3], u.at[5], pc),
        'cd': lambda: rdma('cd', u.at[6], u.at[7], pc),
        'icx': lambda: rdma('icx', info.at[2], info.at[4], pc),
        'icy': lambda: rdma('icy', info.at[3], info.at[5], pc),
        'icd': lambda: rdma('icd', info.at[6], info.at[7], pc),
    }
    for key in ag:
        specs.setdefault(key, len(specs))

    def rs(name, c):
        key = (name, c)
        if name == 'c':
            return rdma(key, pp.at[c, pl.ds(4, 4)], rc.at[c], pc)
        if name == 'xa':
            return rdma(key, pp.at[c, 1, 0], r1.at[c, 0], px)
        if name == 'xb':
            return rdma(key, pp.at[c, 3, 0], r1.at[c, 1], px)
        if name == 'ya':
            return rdma(key, pp.at[c, 2, 1], r1.at[c, 2], py)
        if name == 'yb':
            return rdma(key, pp.at[c, 3, 1], r1.at[c, 3], py)
        if name == 'y2':
            return rdma(key, pp.at[c, 2, 0], r2.at[c, 0], py)
        return rdma(key, pp.at[c, 1, 1], r2.at[c, 1], px)

    def rs_core(c):
        rs('c', c).start()

    def rs_first(c):
        rs('c', c).wait_recv()
        for q in (3, 1, 2, 0):
            pp[c, q] = pp[c, q] + rc[c, q]
        for name in ('xb', 'yb', 'xa', 'ya'):
            rs(name, c).start()

    def rs_second(c):
        rs('xb', c).wait_recv()
        pp[c, 2, 0] = pp[c, 2, 0] + r1[c, 1]
        rs('y2', c).start()
        rs('yb', c).wait_recv()
        pp[c, 1, 1] = pp[c, 1, 1] + r1[c, 3]
        rs('x2', c).start()

    def rs_last(c):
        lo = slice(c * CW, c * CW + HW)
        hi = slice(c * CW + HW, (c + 1) * CW)
        rs('xa', c).wait_recv()
        rs('y2', c).wait_recv()
        out[0, :, lo] = (fs[:, lo] + ((pp[c, 0, 0] + r1[c, 0]) + r2[c, 0])).astype(bf16)
        rs('ya', c).wait_recv()
        rs('x2', c).wait_recv()
        out[0, :, hi] = (fs[:, hi] + ((pp[c, 0, 1] + r1[c, 2]) + r2[c, 1])).astype(bf16)

    barrier = pltpu.get_barrier_semaphore()
    for to in (px, py, pd, pc):
        pl.semaphore_signal(barrier, inc=1, device_id=to, device_id_type=MESH)
    a_copy('k', 0, 0).start()
    a_copy('v', 0, 1).start()
    for i in range(NA - 2):
        a_copy('q', i, 2 + i).start()
    for i in range(NB):
        b_copy('wo', i, i).start()

    def norms(i, _):
        rows = pl.ds(pl.multiple_of(i * 16, 16), 16)
        xf = h0[0, rows, :].astype(f32)
        xr = xf * lax.rsqrt(jnp.mean(xf * xf, axis=-1, keepdims=True) + EPS)
        un = (xr * nm[...].astype(f32)).astype(bf16)
        u[0, 0, rows, :] = un[:, :D // 2]
        u[0, 1, rows, :] = un[:, D // 2:]
        xz[rows, :] = (xr * na[...].astype(f32)).astype(bf16)
        return 0

    lax.fori_loop(0, T // 16, norms, 0)
    pl.semaphore_wait(barrier, 4)
    for key in ('x0', 'y1', 'c', 'x1', 'y0'):
        ag[key]().start()

    logits = _dot(u[0, 0], wr[pl.ds(0, D // 2), :]) + _dot(u[0, 1], wr[pl.ds(D // 2, D // 2), :])
    lt = logits.T
    idt = idx[0].astype(f32).T
    slt = slot[0].astype(f32).T
    ex = lax.broadcasted_iota(jnp.int32, (T, T), 0).astype(f32)
    sel = jnp.concatenate(
        [jnp.sum(jnp.where(ex == idt[j:j + 1, :], lt, 0.0), axis=0, keepdims=True) for j in range(TOP)], axis=0)
    gate = jnp.exp(sel - jnp.max(sel, axis=0, keepdims=True))
    gate = gate / jnp.sum(gate, axis=0, keepdims=True)
    info[0, pl.ds(0, TOP), :] = idt * float(CAP) + slt
    info[0, pl.ds(TOP, TOP), :] = gate

    cs, sn = cos[...], sin[...]

    def rope(v):
        return (v * cs + pltpu.roll(v, HEAD // 2, 1) * sn).astype(bf16)

    a_copy('k', 0, 0).wait()
    kf = _dot(xz[...], ra[0, :, pl.ds(0, QT)])
    a_copy('q', 2, 0).start()
    for n in range(4):
        kk[n] = rope(kf[:, n * HEAD:(n + 1) * HEAD])
    for key in ('ix', 'iy', 'id', 'ic'):
        ag[key]().start()
    a_copy('v', 0, 1).wait()
    vf = _dot(xz[...], ra[1, :, pl.ds(0, QT)])
    a_copy('q', 3, 1).start()
    for n in range(4):
        vv[n] = vf[:, n * HEAD:(n + 1) * HEAD].astype(bf16)
    causal = lax.broadcasted_iota(jnp.int32, (T, T), 0) >= lax.broadcasted_iota(jnp.int32, (T, T), 1)

    def q_step(i, _):
        t = 2 + i
        s = lax.rem(t, NA)
        a_copy('q', i, s).wait()
        qf = _dot(xz[...], ra[s, :, pl.ds(0, QT)])
        a_start(t + NA, 2 + NA, A_FF1 + NA)
        kg, vg = kk[i // 2], vv[i // 2]
        for n in range(4):
            qh = rope(qf[:, n * HEAD:(n + 1) * HEAD])
            sc = lax.dot_general(qh, kg, (((1,), (1,)), ((), ())), preferred_element_type=f32) * HEAD ** -0.5
            sc = jnp.where(causal, sc, -jnp.inf)
            p = jnp.exp(sc - jnp.max(sc, axis=-1, keepdims=True))
            p = (p * (1.0 / jnp.sum(p, axis=-1, keepdims=True))).astype(bf16)
            g[i, :, n * HEAD:(n + 1) * HEAD] = _dot(p, vg).astype(bf16)
        return 0

    lax.fori_loop(0, NQ, q_step, 0)

    ag['x0']().wait_recv()
    ag['d0']().start()
    ag['y1']().wait_recv()
    ag['d1']().start()

    def wo_step(n, _):
        cols = pl.ds(pl.multiple_of(n * CW, CW), CW)
        acc = h0[0, :, cols].astype(f32)
        prod = None
        for half in range(2):
            t = 2 * n + half
            s = lax.rem(t, NB)
            b_copy('wo', t, s).wait()
            for i in range(4):
                term = _dot(g[half * 4 + i, :, pl.ds(0, QT)], rb[s, i, pl.ds(0, QT), :])
                prod = term if prod is None else prod + term
            b_start(t + NB, NB, B_EXP + NB)
        ar[:, cols] = (acc + prod).astype(bf16)
        return 0

    lax.fori_loop(0, D // CW, wo_step, 0)

    def znorm(i, _):
        rows = pl.ds(pl.multiple_of(i * 16, 16), 16)
        xf = ar[rows, :].astype(f32)
        xr = xf * lax.rsqrt(jnp.mean(xf * xf, axis=-1, keepdims=True) + EPS)
        xz[rows, :] = (xr * nf[...].astype(f32)).astype(bf16)
        return 0

    lax.fori_loop(0, T // 16, znorm, 0)

    for key in ('ix', 'iy', 'id', 'x1', 'y0'):
        ag[key]().wait_recv()
    for key in ('icx', 'icy', 'icd', 'cx', 'cy'):
        ag[key]().start()

    def gated(lhs, t, kinds, i, hi):
        s1, s3 = lax.rem(t, NA), lax.rem(t + 1, NA)
        a_copy(kinds[0], i, s1).wait()
        h1 = _dot(lhs, ra[s1])
        a_copy(kinds[1], i, s3).wait()
        h3 = _dot(lhs, ra[s3])
        for k in (0, 1):
            a_start(t + NA + k, *hi)
        return (h1 * jax.nn.sigmoid(h1) * h3).astype(bf16)

    def ffn1(i, _):
        g[i] = gated(xz[...], A_FF1 + 2 * i, ('w1', 'w3'), i, (A_FF1 + NA, A_EXP + NA))
        return 0

    lax.fori_loop(0, N1, ffn1, 0)

    base = ((ep * 32 + e0) * CAP).astype(f32)

    def build(r, _):
        for half in range(2):
            row = lax.broadcasted_iota(jnp.int32, (T, T), 0).astype(f32) + (base + float(half * T))
            w = jnp.zeros((T, T), f32)
            d = jnp.zeros((T, T), f32)
            for j in range(TOP):
                hit = row == info[r, pl.ds(j, 1), :]
                w = jnp.where(hit, info[r, pl.ds(TOP + j, 1), :], w)
                d = jnp.where(hit, 1.0, d)
            wt = w.T
            hi = wt.astype(bf16)
            rest = wt - hi.astype(f32)
            mid = rest.astype(bf16)
            low = (rest - mid.astype(f32)).astype(bf16)
            for n, part in enumerate((hi, mid, low)):
                ws[r, pl.ds(n * T, T), half * T:(half + 1) * T] = part
            db = d.astype(bf16)
            for c in range(4):
                rows = _dot(db, u[r, c // 2, :, (c % 2) * 512:(c % 2 + 1) * 512]).astype(bf16)
                x[pl.ds(half * 8, 8), pl.ds(pl.multiple_of(r * CAP, CAP), CAP), c * 512:(c + 1) * 512] = (
                    rows.reshape(8, CAP, 512))
        return 0

    for key in ('d0', 'd1'):
        ag[key]().wait_recv()
    ag['cd']().start()
    for key in ('ic', 'icx', 'icy', 'icd', 'c', 'cx', 'cy', 'cd'):
        ag[key]().wait_recv()
    lax.fori_loop(0, 8, build, 0)

    def experts(e, _):
        x[e, :, :FE] = gated(x[e], A_EXP + 2 * e, ('e1', 'e3'), e, (A_EXP + NA, A_FF2 + NA))
        return 0

    lax.fori_loop(0, EL, experts, 0)

    YC = 1024

    def chunk(c):
        def part(k, _):
            t = B_EXP + 4 * c + k
            s = lax.rem(t, NB)
            b_copy('e2', 4 * c + k, s).wait()
            for i in range(4):
                x[4 * k + i, :, YC:YC + CW] = _dot(x[4 * k + i, :, :FE], rb[s, i]).astype(bf16)
            b_start(t + NB, B_EXP + NB, B_W2 + NB)
            return 0

        if c == 0:
            lax.fori_loop(0, 4, part, 0)
        else:
            lax.fori_loop(0, 2, part, 0)
            rs_first(c - 1)
            lax.fori_loop(2, 4, part, 0)

        def combine(q, _):
            core, yy, xx = q // 4, lax.rem(q // 2, 2), lax.rem(q, 2)
            r = jnp.where(xx * yy == 1, 6 + core, jnp.where(xx + yy == 0, core, 1 + xx + 2 * yy + 2 * core))
            yr = x[:, pl.ds(pl.multiple_of(r * CAP, CAP), CAP), YC:YC + CW].reshape(2 * T, CW)
            three = _dot(ws[r], yr)
            m = (three[:T] + three[T:2 * T]) + three[2 * T:]
            pp[c, q, 0] = m[:, :HW]
            pp[c, q, 1] = m[:, HW:]
            return 0

        lax.fori_loop(0, 8, combine, 0)
        rs_core(c)

    for c in range(NC):
        chunk(c)

    def ffn2(i, _):
        g[i] = gated(xz[...], A_FF2 - 2 * N1 + 2 * i, ('w1', 'w3'), i, (A_FF2 + NA, A_END))
        for at, fn in ((N1, lambda: rs_second(0)), (N1 + 1, lambda: rs_first(NC - 1)), (N1 + 3, lambda: rs_second(1))):
            @pl.when(i == at)
            def _():
                fn()
        return 0

    lax.fori_loop(N1, NF, ffn2, 0)

    def w2_step(n, _):
        cols = pl.ds(pl.multiple_of(n * CW, CW), CW)
        prod = None
        for half in range(2):
            t = B_W2 + 2 * n + half
            s = lax.rem(t, NB)
            b_copy('w2', 2 * n + half, s).wait()
            for i in range(4):
                term = _dot(g[half * 4 + i], rb[s, i])
                prod = term if prod is None else prod + term
            b_start(t + NB, B_W2 + NB, B_END)
        fs[:, cols] = ar[:, cols].astype(f32) + prod
        return 0

    lax.fori_loop(0, 2, w2_step, 0)
    rs_second(2)
    lax.fori_loop(2, 4, w2_step, 0)
    rs_second(3)
    for c in range(NC):
        rs_last(c)
    for key in ag:
        ag[key]().wait_send()
    for c in range(NC):
        for name in ('c', 'xa', 'xb', 'ya', 'yb', 'y2', 'x2'):
            rs(name, c).wait_send()


def solution(mesh):
    ang = (np.arange(T, dtype=np.float32)[:, None]
           * (ROPE_BASE ** (-2.0 * np.arange(HEAD // 2) / HEAD)).astype(np.float32)[None, :])
    cos = np.cos(ang.astype(np.float64)).astype(np.float32)
    sin = np.sin(ang.astype(np.float64)).astype(np.float32)
    cos2 = np.concatenate([cos, cos], axis=1)
    sin2 = np.concatenate([-sin, sin], axis=1)
    ncopies = 17 + 7 * NC

    def local(h0, idx, slot, na, wq, wk, wv, wo, nf, w1, w3, w2, nm, wr, ue1, ue3, ue2):
        vm = pl.BlockSpec(memory_space=pltpu.VMEM)
        hb = pl.BlockSpec(memory_space=pl.ANY)
        return pl.pallas_call(
            _kernel,
            out_shape=jax.ShapeDtypeStruct(h0.shape, bf16),
            in_specs=[vm] * 9 + [hb] * 10,
            out_specs=vm,
            scratch_shapes=[
                pltpu.VMEM((T, D), bf16),
                pltpu.VMEM((T, D), bf16),
                pltpu.VMEM((T, D), f32),
                pltpu.VMEM((8, 2, T, D // 2), bf16),
                pltpu.VMEM((8, 2 * TOP, T), f32),
                pltpu.VMEM((8, 3 * T, 2 * T), bf16),
                pltpu.VMEM((EL, T, D), bf16),
                pltpu.VMEM((4, T, HEAD), bf16),
                pltpu.VMEM((4, T, HEAD), bf16),
                pltpu.VMEM((NF, T, FE), bf16),
                pltpu.VMEM((NC, 8, 2, T, HW), f32),
                pltpu.VMEM((NC, 4, 2, T, HW), f32),
                pltpu.VMEM((NC, 4, T, HW), f32),
                pltpu.VMEM((NC, 2, T, HW), f32),
                pltpu.VMEM((NA, D, FE), bf16),
                pltpu.VMEM((NB, 4, FE, CW), bf16),
                pltpu.SemaphoreType.DMA((NA,)),
                pltpu.SemaphoreType.DMA((NB,)),
                pltpu.SemaphoreType.DMA((ncopies,)),
                pltpu.SemaphoreType.DMA((ncopies,)),
            ],
            compiler_params=pltpu.CompilerParams(collective_id=0, has_side_effects=True,
                                                 vmem_limit_bytes=67043328),
            name='scmoe',
        )(h0, idx, slot, na.reshape(1, D), nf.reshape(1, D), nm.reshape(1, D),
          jnp.asarray(cos2), jnp.asarray(sin2), wr, wq, wk, wv, wo.reshape(8, QT, D),
          w1, w3, w2.reshape(8, FE, D), ue1, ue3, ue2)

    rows = P(('dp', 'ep'))
    in_specs = (rows,) * 3 + (P(),) * 11 + (P('ep'),) * 3
    return jax.shard_map(local, mesh=mesh, in_specs=in_specs, out_specs=rows, check_vma=False)
```

time: 413 us -> 121 us (0.29)
  matrix products: 170 us -> 0 us
  Pallas kernels: 0 us -> 112 us
  waiting for transfers between devices: 111 us -> 0 us
  local copies, waits for them, and re-layouts: 95.9 us -> 8.55 us
  other arithmetic: 22.4 us -> 0 us
  starting transfers between devices: 11.8 us -> 0 us
    dot_general x12 -> x0, matrix products: 170 us -> none  [the longest x1 38.8 us: _experts(): h3 = jnp.einsum('ecd,edf->ecf', x, ue3, preferred_element_type=f32)]
    pallas_call x0 -> x1, Pallas kernels: none -> 112 us  [local(): pl.pallas_call(_kernel, out_shape=jax.ShapeDtypeStruct(h0.shape, bf16), i...]
    all_to_all x2 -> x0, waiting for transfers between devices: 111 us -> none  [the longest x1 61.5 us: local(): recv = lax.all_to_all(send, 'ep', 0, 0, tiled=True)]
    gather x6 -> x0, local copies, waits for them, and re-layouts: 43.5 us -> none  [the longest x1 25.5 us: local(): yg = back[ix, sl]]
    dot_general x2 -> x0, local copies, waits for them, and re-layouts: 25.5 us -> none  [the longest x1 22.6 us: _dense(): jnp.dot(x, wq, preferred_element_type=f32).reshape(b, s, nh, HEAD)]
    transpose x2 -> x0, local copies, waits for them, and re-layouts: 16.5 us -> none  [the longest x1 8.25 us: local(): recv.reshape(G, el, cap, d).transpose(1, 0, 2, 3).reshape(el, G * cap, d)]
    all_to_all x2 -> x0, starting transfers between devices: 11.8 us -> none  [the longest x1 5.96 us: local(): recv = lax.all_to_all(send, 'ep', 0, 0, tiled=True)]
    reduce_sum x4 -> x0, other arithmetic: 9.31 us -> none  [the longest x1 7.55 us: local(): m = jnp.sum(g[..., None] * yg.astype(f32), axis=1)]
  transfers between devices with their start and end apart: 2 -> 0, of which waited for: 2 -> 0; matrix products, arithmetic and copies ran while one was open for 18% -> 0% of each run, Pallas kernels for 0% -> 0%
where the time goes in v1:
time: 121 us; the launch traced here: 120 us
  Pallas kernels  112 us (93%)
  local copies, waits for them, and re-layouts  8.55 us (7%)
    pallas_call x1, Pallas kernels, local(): pl.pallas_call(_kernel, out_shape=jax.ShapeDtypeStruct(h0.shape, bf16), i...  112 us
    unnamed x3, local copies, waits for them, and re-layouts  4.7 us

profile of v1, /device:TPU:0, one launch (start us, length us, event | category | flops | bytes accessed | tf_op | source)
XLA Modules:
  0.0 120.2 jit_solution(12026295411484128482)
XLA Ops:
  0.0 1.3 %reshape.15.na = bf16[1,2048]{1,0:T(2,128)(2,1)} reshape(bf16[2048]{0:T(1024)(128)(2,1)} %param.22) | data formatting | bytes 8192 | tf_op jit(solution)/shard_map/reshape | solution.py:460
  1.3 1.3 %reshape.16.nf = bf16[1,2048]{1,0:T(2,128)(2,1)} reshape(bf16[2048]{0:T(1024)(128)(2,1)} %param.27) | data formatting | bytes 8192 | tf_op jit(solution)/shard_map/reshape | solution.py:460
  2.6 1.3 %reshape.17.nm = bf16[1,2048]{1,0:T(2,128)(2,1)} reshape(bf16[2048]{0:T(1024)(128)(2,1)} %param.31) | data formatting | bytes 8192 | tf_op jit(solution)/shard_map/reshape | solution.py:460
  3.9 1.4 %copy.20.idx = s32[1,128,8]{2,1,0:T(8,128)} copy(s32[1,128,8]{1,2,0:T(8,128)} %param.20) | data formatting | bytes 8192 | tf_op args[1]
  5.3 1.4 %copy.21.slot = s32[1,128,8]{2,1,0:T(8,128)} copy(s32[1,128,8]{1,2,0:T(8,128)} %param.21) | data formatting | bytes 8192 | tf_op args[2]
  6.7 111.6 %scmoe.1 = bf16[1,128,2048]{2,1,0:T(8,128)(2,1)} custom-call(bf16[1,128,2048]{2,1,0:T(8,128)(2,1)} %h0.1, s32[1,128,8]{2,1,0:T(8,128)} %copy.20.idx, s32[1,128,8]{2,1,0:T(8,128)} %copy.21.slot, bf16[1,2048]{1,0:T(2,128)(2,1)} %reshape.15.na, bf16[1,2048]{1,0:T(2,128)(2,1)} %reshape.16.nf, bf16[1,2048]{1,0:T(2,128)(2,1)} %reshape.17.nm, ...), custom_call_target="tpu_custom_call" | custom-call | tf_op jit(solution)/shard_map/scmoe/pallas_call | solution.py:430
  118.3 1.9 %copy.23 = bf16[1,128,2048]{2,1,0:T(8,128)(2,1)} copy(bf16[1,128,2048]{2,1,0:T(8,128)(2,1)} %scmoe.1) | data formatting | bytes 1048576

commit v2 on v1

--- a/solution.py
+++ b/solution.py
@@ -22,8 +22,10 @@
 NA = 4
 NB = 4
 NQ = 8
+Q_FWD = 2
+PLACE = (0, 2, 3, 6, 1, 4, 5, 7)
 NF = FF // FE
-N1 = 4
+N1 = 1
 A_FF1 = 2 + NQ
 A_EXP = A_FF1 + 2 * N1
 A_FF2 = A_EXP + 2 * EL
@@ -40,7 +42,7 @@
 
 
 def _kernel(h0, idx, slot, na, nf, nm, cos, sin, wr, wq, wk, wv, wo, w1, w3, w2, ue1, ue3, ue2, out,
-            xz, ar, fs, u, info, ws, x, kk, vv, g, pp, rc, r1, r2, ra, rb,
+            xz, ar, fs, qa, qb, u, info, ws, x, kk, vv, g, pp, rc, r1, r2, ra, rb,
             sem_a, sem_b, send, recv):
     dp, ep = lax.axis_index('dp'), lax.axis_index('ep')
     px = (dp, lax.rem(ep + 2, 4))
@@ -137,8 +139,9 @@
 
     def rs(name, c):
         key = (name, c)
-        if name == 'c':
-            return rdma(key, pp.at[c, pl.ds(4, 4)], rc.at[c], pc)
+        if name[0] == 'c':
+            n = int(name[1])
+            return rdma(key, pp.at[c, 4 + n], rc.at[c, n], pc)
         if name == 'xa':
             return rdma(key, pp.at[c, 1, 0], r1.at[c, 0], px)
         if name == 'xb':
@@ -151,15 +154,12 @@
             return rdma(key, pp.at[c, 2, 0], r2.at[c, 0], py)
         return rdma(key, pp.at[c, 1, 1], r2.at[c, 1], px)
 
-    def rs_core(c):
-        rs('c', c).start()
-
     def rs_first(c):
-        rs('c', c).wait_recv()
         for q in (3, 1, 2, 0):
+            rs('c%d' % q, c).wait_recv()
             pp[c, q] = pp[c, q] + rc[c, q]
-        for name in ('xb', 'yb', 'xa', 'ya'):
-            rs(name, c).start()
+            for name in ((), ('xa',), ('ya',), ('xb', 'yb'))[q]:
+                rs(name, c).start()
 
     def rs_second(c):
         rs('xb', c).wait_recv()
@@ -193,21 +193,21 @@
         rows = pl.ds(pl.multiple_of(i * 16, 16), 16)
         xf = h0[0, rows, :].astype(f32)
         xr = xf * lax.rsqrt(jnp.mean(xf * xf, axis=-1, keepdims=True) + EPS)
-        un = (xr * nm[...].astype(f32)).astype(bf16)
+        un = (xr * nm[...].astype(f32)[None, :]).astype(bf16)
         u[0, 0, rows, :] = un[:, :D // 2]
         u[0, 1, rows, :] = un[:, D // 2:]
-        xz[rows, :] = (xr * na[...].astype(f32)).astype(bf16)
-        return 0
-
-    lax.fori_loop(0, T // 16, norms, 0)
+        xz[rows, :] = (xr * na[...].astype(f32)[None, :]).astype(bf16)
+        return 0
+
+    lax.fori_loop(0, T // 16, norms, 0, unroll=4)
     pl.semaphore_wait(barrier, 4)
     for key in ('x0', 'y1', 'c', 'x1', 'y0'):
         ag[key]().start()
 
     logits = _dot(u[0, 0], wr[pl.ds(0, D // 2), :]) + _dot(u[0, 1], wr[pl.ds(D // 2, D // 2), :])
     lt = logits.T
-    idt = idx[0].astype(f32).T
-    slt = slot[0].astype(f32).T
+    idt = idx[0].astype(f32)
+    slt = slot[0].astype(f32)
     ex = lax.broadcasted_iota(jnp.int32, (T, T), 0).astype(f32)
     sel = jnp.concatenate(
         [jnp.sum(jnp.where(ex == idt[j:j + 1, :], lt, 0.0), axis=0, keepdims=True) for j in range(TOP)], axis=0)
@@ -235,28 +235,45 @@
         vv[n] = vf[:, n * HEAD:(n + 1) * HEAD].astype(bf16)
     causal = lax.broadcasted_iota(jnp.int32, (T, T), 0) >= lax.broadcasted_iota(jnp.int32, (T, T), 1)
 
-    def q_step(i, _):
-        t = 2 + i
-        s = lax.rem(t, NA)
+    def q_dot(i, dst):
+        s = lax.rem(2 + i, NA)
         a_copy('q', i, s).wait()
-        qf = _dot(xz[...], ra[s, :, pl.ds(0, QT)])
-        a_start(t + NA, 2 + NA, A_FF1 + NA)
+        dst[...] = _dot(xz[...], ra[s, :, pl.ds(0, QT)])
+        a_start(2 + i + NA, 2 + NA, A_FF1 + NA)
+
+    def q_heads(i, src):
         kg, vg = kk[i // 2], vv[i // 2]
+        qs = jnp.concatenate([rope(src[:, n * HEAD:(n + 1) * HEAD]) for n in range(4)], axis=0)
+        sc = lax.dot_general(qs, kg, (((1,), (1,)), ((), ())), preferred_element_type=f32) * HEAD ** -0.5
+        ps = []
         for n in range(4):
-            qh = rope(qf[:, n * HEAD:(n + 1) * HEAD])
-            sc = lax.dot_general(qh, kg, (((1,), (1,)), ((), ())), preferred_element_type=f32) * HEAD ** -0.5
-            sc = jnp.where(causal, sc, -jnp.inf)
-            p = jnp.exp(sc - jnp.max(sc, axis=-1, keepdims=True))
-            p = (p * (1.0 / jnp.sum(p, axis=-1, keepdims=True))).astype(bf16)
-            g[i, :, n * HEAD:(n + 1) * HEAD] = _dot(p, vg).astype(bf16)
-        return 0
-
-    lax.fori_loop(0, NQ, q_step, 0)
-
-    ag['x0']().wait_recv()
-    ag['d0']().start()
-    ag['y1']().wait_recv()
-    ag['d1']().start()
+            sm = jnp.where(causal, sc[n * T:(n + 1) * T], -jnp.inf)
+            p = jnp.exp(sm - jnp.max(sm, axis=-1, keepdims=True))
+            ps.append((p * (1.0 / jnp.sum(p, axis=-1, keepdims=True))).astype(bf16))
+        o = _dot(jnp.concatenate(ps, axis=0), vg)
+        for n in range(4):
+            g[i, :, n * HEAD:(n + 1) * HEAD] = o[n * T:(n + 1) * T].astype(bf16)
+
+    def q_pair(k, _):
+        q_dot(2 * k + 1, qb)
+        q_heads(2 * k, qa)
+
+        @pl.when(k == Q_FWD)
+        def _():
+            ag['x0']().wait_recv()
+            ag['d0']().start()
+            ag['y1']().wait_recv()
+            ag['d1']().start()
+
+        q_dot(2 * k + 2, qa)
+        q_heads(2 * k + 1, qb)
+        return 0
+
+    q_dot(0, qa)
+    lax.fori_loop(0, NQ // 2 - 1, q_pair, 0)
+    q_dot(NQ - 1, qb)
+    q_heads(NQ - 2, qa)
+    q_heads(NQ - 1, qb)
 
     def wo_step(n, _):
         cols = pl.ds(pl.multiple_of(n * CW, CW), CW)
@@ -279,10 +296,10 @@
         rows = pl.ds(pl.multiple_of(i * 16, 16), 16)
         xf = ar[rows, :].astype(f32)
         xr = xf * lax.rsqrt(jnp.mean(xf * xf, axis=-1, keepdims=True) + EPS)
-        xz[rows, :] = (xr * nf[...].astype(f32)).astype(bf16)
-        return 0
-
-    lax.fori_loop(0, T // 16, znorm, 0)
+        xz[rows, :] = (xr * nf[...].astype(f32)[None, :]).astype(bf16)
+        return 0
+
+    lax.fori_loop(0, T // 16, znorm, 0, unroll=4)
 
     for key in ('ix', 'iy', 'id', 'x1', 'y0'):
         ag[key]().wait_recv()
@@ -330,12 +347,16 @@
                     rows.reshape(8, CAP, 512))
         return 0
 
+    for key in ('ic', 'icx', 'icy', 'c', 'cx', 'cy'):
+        ag[key]().wait_recv()
+    lax.fori_loop(0, 6, build, 0)
     for key in ('d0', 'd1'):
         ag[key]().wait_recv()
     ag['cd']().start()
-    for key in ('ic', 'icx', 'icy', 'icd', 'c', 'cx', 'cy', 'cd'):
+    build(6, 0)
+    for key in ('icd', 'cd'):
         ag[key]().wait_recv()
-    lax.fori_loop(0, 8, build, 0)
+    build(7, 0)
 
     def experts(e, _):
         x[e, :, :FE] = gated(x[e], A_EXP + 2 * e, ('e1', 'e3'), e, (A_EXP + NA, A_FF2 + NA))
@@ -362,25 +383,23 @@
             rs_first(c - 1)
             lax.fori_loop(2, 4, part, 0)
 
-        def combine(q, _):
-            core, yy, xx = q // 4, lax.rem(q // 2, 2), lax.rem(q, 2)
-            r = jnp.where(xx * yy == 1, 6 + core, jnp.where(xx + yy == 0, core, 1 + xx + 2 * yy + 2 * core))
-            yr = x[:, pl.ds(pl.multiple_of(r * CAP, CAP), CAP), YC:YC + CW].reshape(2 * T, CW)
+        for q in (7, 5, 6, 4, 3, 1, 2, 0):
+            r = PLACE[q]
+            yr = x[:, r * CAP:(r + 1) * CAP, YC:YC + CW].reshape(2 * T, CW)
             three = _dot(ws[r], yr)
             m = (three[:T] + three[T:2 * T]) + three[2 * T:]
             pp[c, q, 0] = m[:, :HW]
             pp[c, q, 1] = m[:, HW:]
-            return 0
-
-        lax.fori_loop(0, 8, combine, 0)
-        rs_core(c)
+            if q >= 4:
+                rs('c%d' % (q - 4), c).start()
 
     for c in range(NC):
         chunk(c)
 
     def ffn2(i, _):
         g[i] = gated(xz[...], A_FF2 - 2 * N1 + 2 * i, ('w1', 'w3'), i, (A_FF2 + NA, A_END))
-        for at, fn in ((N1, lambda: rs_second(0)), (N1 + 1, lambda: rs_first(NC - 1)), (N1 + 3, lambda: rs_second(1))):
+        for at, fn in ((N1, lambda: rs_first(NC - 1)), (N1 + 1, lambda: rs_second(0)), (N1 + 3, lambda: rs_second(1)),
+                       (NF - 1, lambda: rs_second(2))):
             @pl.when(i == at)
             def _():
                 fn()
@@ -402,16 +421,14 @@
         fs[:, cols] = ar[:, cols].astype(f32) + prod
         return 0
 
-    lax.fori_loop(0, 2, w2_step, 0)
-    rs_second(2)
-    lax.fori_loop(2, 4, w2_step, 0)
+    lax.fori_loop(0, 4, w2_step, 0)
     rs_second(3)
     for c in range(NC):
         rs_last(c)
     for key in ag:
         ag[key]().wait_send()
     for c in range(NC):
-        for name in ('c', 'xa', 'xb', 'ya', 'yb', 'y2', 'x2'):
+        for name in ('c0', 'c1', 'c2', 'c3', 'xa', 'xb', 'ya', 'yb', 'y2', 'x2'):
             rs(name, c).wait_send()
 
 
@@ -422,7 +439,7 @@
     sin = np.sin(ang.astype(np.float64)).astype(np.float32)
     cos2 = np.concatenate([cos, cos], axis=1)
     sin2 = np.concatenate([-sin, sin], axis=1)
-    ncopies = 17 + 7 * NC
+    ncopies = 17 + 10 * NC
 
     def local(h0, idx, slot, na, wq, wk, wv, wo, nf, w1, w3, w2, nm, wr, ue1, ue3, ue2):
         vm = pl.BlockSpec(memory_space=pltpu.VMEM)
@@ -436,6 +453,8 @@
                 pltpu.VMEM((T, D), bf16),
                 pltpu.VMEM((T, D), bf16),
                 pltpu.VMEM((T, D), f32),
+                pltpu.VMEM((T, QT), f32),
+                pltpu.VMEM((T, QT), f32),
                 pltpu.VMEM((8, 2, T, D // 2), bf16),
                 pltpu.VMEM((8, 2 * TOP, T), f32),
                 pltpu.VMEM((8, 3 * T, 2 * T), bf16),
@@ -457,7 +476,7 @@
             compiler_params=pltpu.CompilerParams(collective_id=0, has_side_effects=True,
                                                  vmem_limit_bytes=67043328),
             name='scmoe',
-        )(h0, idx, slot, na.reshape(1, D), nf.reshape(1, D), nm.reshape(1, D),
+        )(h0, jnp.swapaxes(idx, 1, 2), jnp.swapaxes(slot, 1, 2), na, nf, nm,
           jnp.asarray(cos2), jnp.asarray(sin2), wr, wq, wk, wv, wo.reshape(8, QT, D),
           w1, w3, w2.reshape(8, FE, D), ue1, ue3, ue2)
 

time: 121 us -> 102 us (0.84)
  Pallas kernels: 112 us -> 99.9 us
  local copies, waits for them, and re-layouts: 8.55 us -> 1.88 us
    pallas_call x1, Pallas kernels: 112 us -> 99.9 us  [local(): pl.pallas_call(_kernel, out_shape=jax.ShapeDtypeStruct(h0.shape, bf16), i...]
    reshape x3 -> x0, local copies, waits for them, and re-layouts: 3.85 us -> none  [the longest x1 1.29 us: local(): na.reshape(1, D)]
    unnamed x3 -> x1, local copies, waits for them, and re-layouts: 4.7 us -> 1.88 us
where the time goes in v2:
time: 102 us
  Pallas kernels  99.9 us (98%)
  local copies, waits for them, and re-layouts  1.88 us (2%)
    pallas_call x1, Pallas kernels, local(): pl.pallas_call(_kernel, out_shape=jax.ShapeDtypeStruct(h0.shape, bf16), i...  99.9 us

profile of v2, /device:TPU:0, one launch (start us, length us, event | category | flops | bytes accessed | tf_op | source)
XLA Modules:
  0.0 101.8 jit_solution(3955694067090478967)
XLA Ops:
  0.0 99.9 %scmoe.1 = bf16[1,128,2048]{2,1,0:T(8,128)(2,1)} custom-call(bf16[1,128,2048]{2,1,0:T(8,128)(2,1)} %h0.1, s32[1,8,128]{2,1,0:T(8,128)} %bitcast.6, s32[1,8,128]{2,1,0:T(8,128)} %bitcast.7, bf16[2048]{0:T(1024)(128)(2,1)} %na.1, bf16[2048]{0:T(1024)(128)(2,1)} %nf.1, bf16[2048]{0:T(1024)(128)(2,1)} %nm.1, f32[128,128]{1,0:T(8,128)} %constant.4.clone.cos, ...), custom_call_target="tpu_custom_call" | custom-call | tf_op jit(solution)/shard_map/scmoe/pallas_call | solution.py:447
  99.9 1.9 %copy.21 = bf16[1,128,2048]{2,1,0:T(8,128)(2,1)} copy(bf16[1,128,2048]{2,1,0:T(8,128)(2,1)} %scmoe.1) | data formatting | bytes 1048576

commit v3 on v2

v3 whole, which is shorter than its diff:
```python
import functools

import jax
import jax.numpy as jnp
import numpy as np
from jax import lax
from jax.experimental import pallas as pl
from jax.experimental.pallas import tpu as pltpu
from jax.sharding import PartitionSpec as P

MESH = pl.DeviceIdType.MESH
HEAD = 128
EPS = 1e-6
ROPE_BASE = 10000.0

T, D, FE, FF, TOP, CAP = 128, 2048, 768, 6144, 8, 16
EL = 16
QT = 512
CW = 512
NC = D // CW
HW = CW // 2
NA = 4
NB = 4
NQ = 8
Q_FWD = 1
E_FWD = (0, 2, 5)
PLACE = (0, 2, 3, 6, 1, 4, 5, 7)
NF = FF // FE
KH = D // 2
A_EXP = 2 + NQ
A_FFN = A_EXP + 2 * EL
A_END = A_FFN + 2 * NF
B_WO = 4 * NC
B_W2 = B_WO + 8
B_END = B_W2 + 8
RC = 16 * NC
R1 = RC + 8 * NC
R2 = R1 + 4 * NC
NBLK = R2 + 2 * NC

f32, bf16 = jnp.float32, jnp.bfloat16


def _dot(a, b):
    return jnp.dot(a, b, preferred_element_type=f32)


def _mult(v):
    return v if isinstance(v, int) else pl.multiple_of(v, CW)


def _kernel(h0, idx, slot, na, nf, nm, cos, sin, wr, wq, wk, wv, wo, w1, w3, w2, ue1, ue3, ue2, out,
            xz, ar, qa, qb, u, info, ws, ds, x, kk, vv, g, big, ra, rb,
            sem_a, sem_b, send, recv, ready):
    dp, ep = lax.axis_index('dp'), lax.axis_index('ep')
    px = (dp, lax.rem(ep + 2, 4))
    py = (1 - dp, ep)
    pd = (1 - dp, lax.rem(ep + 2, 4))
    pc = (dp, ep + 1 - 2 * lax.rem(ep, 2))
    e0 = dp * EL

    def a_copy(kind, i, s):
        if kind == 'k':
            return pltpu.make_async_copy(wk, ra.at[s, :, pl.ds(0, QT)], sem_a.at[s])
        if kind == 'v':
            return pltpu.make_async_copy(wv, ra.at[s, :, pl.ds(0, QT)], sem_a.at[s])
        if kind == 'q':
            c = pl.multiple_of(i * QT, QT)
            return pltpu.make_async_copy(wq.at[:, pl.ds(c, QT)], ra.at[s, :, pl.ds(0, QT)], sem_a.at[s])
        if kind in ('w1', 'w3'):
            c = pl.multiple_of(i * FE, FE)
            return pltpu.make_async_copy((w1 if kind == 'w1' else w3).at[:, pl.ds(c, FE)], ra.at[s], sem_a.at[s])
        raise ValueError(kind)

    def e_start(t, s):
        k = t - A_EXP
        first = k < EL
        e = e0 + jnp.where(first, k, 2 * EL - 1 - k)
        rows = pl.ds(pl.multiple_of(jnp.where(first, 0, KH), KH), KH)
        pltpu.make_async_copy(ue1.at[e, rows, :], ra.at[s, pl.ds(0, KH), :], sem_a.at[s]).start()
        pltpu.make_async_copy(ue3.at[e, rows, :], ra.at[s, pl.ds(KH, KH), :], sem_a.at[s]).start()

    def e_wait(s):
        pltpu.make_async_copy(ue1.at[e0], ra.at[s], sem_a.at[s]).wait()

    def a_start(t, lo, hi):
        s = lax.rem(t, NA)
        if lo < A_EXP:
            @pl.when(t < A_EXP)
            def _():
                a_copy('q', t - 2, s).start()
        if lo < A_FFN and hi > A_EXP:
            @pl.when((t >= A_EXP) & (t < A_FFN))
            def _():
                e_start(t, s)
        if hi > A_FFN:
            for par in (0, 1):
                @pl.when((t >= A_FFN) & (t < A_END) & (lax.rem(t - A_FFN, 2) == par))
                def _():
                    a_copy(('w1', 'w3')[par], (t - A_FFN) // 2, s).start()

    def b_copy(kind, i, s):
        if kind == 'wo':
            return pltpu.make_async_copy(
                wo.at[pl.ds(i % 2 * 4, 4), :, pl.ds(_mult(i // 2 * CW), CW)],
                rb.at[s, :, pl.ds(0, QT), :], sem_b.at[s])
        if kind == 'w2':
            return pltpu.make_async_copy(
                w2.at[pl.ds(i % 2 * 4, 4), :, pl.ds(_mult(i // 2 * CW), CW)],
                rb.at[s], sem_b.at[s])
        return pltpu.make_async_copy(
            ue2.at[pl.ds(e0 + i % 4 * 4, 4), :, pl.ds(_mult(i // 4 * CW), CW)],
            rb.at[s], sem_b.at[s])

    def b_start(t, lo, hi):
        s = lax.rem(t, NB)
        for first, last, name in ((0, B_WO, 'e2'), (B_WO, B_W2, 'wo'), (B_W2, B_END, 'w2')):
            a, b = max(first, lo), min(last, hi)
            if a >= b:
                continue

            @pl.when((t >= a) & (t < b))
            def _():
                b_copy(name, t - first, s).start()

    specs = {}

    def rdma(key, src, dst, to):
        i = specs.setdefault(key, len(specs))
        return pltpu.make_async_remote_copy(src_ref=src, dst_ref=dst, send_sem=send.at[i], recv_sem=recv.at[i],
                                            device_id=to, device_id_type=MESH)

    ag = {
        'ix': lambda: rdma('ix', info.at[0], info.at[2], px),
        'iy': lambda: rdma('iy', info.at[0], info.at[3], py),
        'id': lambda: rdma('id', info.at[0], info.at[6], pd),
        'ic': lambda: rdma('ic', info.at[0], info.at[1], pc),
        'c0': lambda: rdma('c0', u.at[0, pl.ds(0, 2)], u.at[1, pl.ds(0, 2)], pc),
        'c1': lambda: rdma('c1', u.at[0, pl.ds(2, 2)], u.at[1, pl.ds(2, 2)], pc),
        'x0': lambda: rdma('x0', u.at[0, 0], u.at[2, 0], px),
        'y0': lambda: rdma('y0', u.at[0, 0], u.at[3, 0], py),
        'x1': lambda: rdma('x1', u.at[0, 1], u.at[2, 1], px),
        'y1': lambda: rdma('y1', u.at[0, 1], u.at[3, 1], py),
        'x2': lambda: rdma('x2', u.at[0, 2], u.at[2, 2], px),
        'y2': lambda: rdma('y2', u.at[0, 2], u.at[3, 2], py),
        'x3': lambda: rdma('x3', u.at[0, 3], u.at[2, 3], px),
        'y3': lambda: rdma('y3', u.at[0, 3], u.at[3, 3], py),
        'd0': lambda: rdma('d0', u.at[2, 0], u.at[6, 0], py),
        'd1': lambda: rdma('d1', u.at[3, 1], u.at[6, 1], px),
        'd2': lambda: rdma('d2', u.at[2, 2], u.at[6, 2], py),
        'd3': lambda: rdma('d3', u.at[3, 3], u.at[6, 3], px),
        'cx0': lambda: rdma('cx0', u.at[2, pl.ds(0, 2)], u.at[4, pl.ds(0, 2)], pc),
        'cx1': lambda: rdma('cx1', u.at[2, pl.ds(2, 2)], u.at[4, pl.ds(2, 2)], pc),
        'cy0': lambda: rdma('cy0', u.at[3, pl.ds(0, 2)], u.at[5, pl.ds(0, 2)], pc),
        'cy1': lambda: rdma('cy1', u.at[3, pl.ds(2, 2)], u.at[5, pl.ds(2, 2)], pc),
        'cd0': lambda: rdma('cd0', u.at[6, pl.ds(0, 2)], u.at[7, pl.ds(0, 2)], pc),
        'cd1': lambda: rdma('cd1', u.at[6, pl.ds(2, 2)], u.at[7, pl.ds(2, 2)], pc),
        'icx': lambda: rdma('icx', info.at[2], info.at[4], pc),
        'icy': lambda: rdma('icy', info.at[3], info.at[5], pc),
        'icd': lambda: rdma('icd', info.at[6], info.at[7], pc),
    }
    for key in ag:
        specs.setdefault(key, len(specs))

    def sums(c, q, half=0):
        return c * 16 + q * 2 + half

    def rs(name, c):
        key = (name, c)
        if name[0] == 'c':
            n = int(name[1])
            return rdma(key, big.at[pl.ds(sums(c, 4 + n), 2)], big.at[pl.ds(RC + c * 8 + n * 2, 2)], pc)
        src, dst, to = {
            'xa': (sums(c, 1, 0), R1 + c * 4, px),
            'xb': (sums(c, 3, 0), R1 + c * 4 + 1, px),
            'ya': (sums(c, 2, 1), R1 + c * 4 + 2, py),
            'yb': (sums(c, 3, 1), R1 + c * 4 + 3, py),
            'y2': (sums(c, 2, 0), R2 + c * 2, py),
            'x2': (sums(c, 1, 1), R2 + c * 2 + 1, px),
        }[name]
        return rdma(key, big.at[src], big.at[dst], to)

    def rs_first(c):
        for q in (3, 1, 2, 0):
            rs('c%d' % q, c).wait_recv()
            for half in range(2):
                k = sums(c, q, half)
                big[k] = big[k] + big[RC + c * 8 + q * 2 + half]
            for name in ((), ('xa',), ('ya',), ('xb', 'yb'))[q]:
                rs(name, c).start()

    def rs_second(c):
        rs('xb', c).wait_recv()
        big[sums(c, 2, 0)] = big[sums(c, 2, 0)] + big[R1 + c * 4 + 1]
        rs('y2', c).start()
        rs('yb', c).wait_recv()
        big[sums(c, 1, 1)] = big[sums(c, 1, 1)] + big[R1 + c * 4 + 3]
        rs('x2', c).start()

    def rs_last(c, f):
        rs('xa', c).wait_recv()
        rs('y2', c).wait_recv()
        m = (big[sums(c, 0, 0)] + big[R1 + c * 4]) + big[R2 + c * 2]
        out[0, :, c * CW:c * CW + HW] = (f[:, :HW] + m).astype(bf16)
        rs('ya', c).wait_recv()
        rs('x2', c).wait_recv()
        m = (big[sums(c, 0, 1)] + big[R1 + c * 4 + 2]) + big[R2 + c * 2 + 1]
        out[0, :, c * CW + HW:(c + 1) * CW] = (f[:, HW:] + m).astype(bf16)

    barrier = pltpu.get_barrier_semaphore()
    for to in (px, py, pd, pc):
        pl.semaphore_signal(barrier, inc=1, device_id=to, device_id_type=MESH)
    a_copy('k', 0, 0).start()
    a_copy('v', 0, 1).start()
    for i in range(NA - 2):
        a_copy('q', i, 2 + i).start()

    def norms(i, _):
        rows = pl.ds(pl.multiple_of(i * 16, 16), 16)
        xf = h0[0, rows, :].astype(f32)
        xr = xf * lax.rsqrt(jnp.mean(xf * xf, axis=-1, keepdims=True) + EPS)
        un = (xr * nm[...].astype(f32)[None, :]).astype(bf16)
        for k in range(4):
            u[0, k, rows, :] = un[:, k * 512:(k + 1) * 512]
        xz[rows, :] = (xr * na[...].astype(f32)[None, :]).astype(bf16)
        return 0

    lax.fori_loop(0, T // 16, norms, 0, unroll=4)
    pl.semaphore_wait(barrier, 4)
    for key in ('x0', 'y1', 'c0', 'x1', 'y0', 'c1'):
        ag[key]().start()

    logits = _dot(u[0, 0], wr[pl.ds(0, 512), :])
    for k in range(1, 4):
        logits = logits + _dot(u[0, k], wr[pl.ds(k * 512, 512), :])
    lt = logits.T
    idt = idx[0].astype(f32)
    slt = slot[0].astype(f32)
    ex = lax.broadcasted_iota(jnp.int32, (T, T), 0).astype(f32)
    sel = jnp.concatenate(
        [jnp.sum(jnp.where(ex == idt[j:j + 1, :], lt, 0.0), axis=0, keepdims=True) for j in range(TOP)], axis=0)
    gate = jnp.exp(sel - jnp.max(sel, axis=0, keepdims=True))
    gate = gate / jnp.sum(gate, axis=0, keepdims=True)
    info[0, pl.ds(0, TOP), :] = idt * float(CAP) + slt
    info[0, pl.ds(TOP, TOP), :] = gate

    cs, sn = cos[...], sin[...]

    def rope(v):
        return (v * cs + pltpu.roll(v, HEAD // 2, 1) * sn).astype(bf16)

    a_copy('k', 0, 0).wait()
    kf = _dot(xz[...], ra[0, :, pl.ds(0, QT)])
    a_copy('q', 2, 0).start()
    for n in range(4):
        kk[n] = rope(kf[:, n * HEAD:(n + 1) * HEAD])
    for key in ('ix', 'iy', 'id', 'ic'):
        ag[key]().start()
    a_copy('v', 0, 1).wait()
    vf = _dot(xz[...], ra[1, :, pl.ds(0, QT)])
    a_copy('q', 3, 1).start()
    for n in range(4):
        vv[n] = vf[:, n * HEAD:(n + 1) * HEAD].astype(bf16)
    causal = lax.broadcasted_iota(jnp.int32, (T, T), 0) >= lax.broadcasted_iota(jnp.int32, (T, T), 1)

    def q_dot(i, dst):
        s = lax.rem(2 + i, NA)
        a_copy('q', i, s).wait()
        dst[...] = _dot(xz[...], ra[s, :, pl.ds(0, QT)])
        a_start(2 + i + NA, 2 + NA, A_EXP + NA)

    def q_heads(i, src):
        kg, vg = kk[i // 2], vv[i // 2]
        qs = jnp.concatenate([rope(src[:, n * HEAD:(n + 1) * HEAD]) for n in range(4)], axis=0)
        sc = lax.dot_general(qs, kg, (((1,), (1,)), ((), ())), preferred_element_type=f32) * HEAD ** -0.5
        ps = []
        for n in range(4):
            sm = jnp.where(causal, sc[n * T:(n + 1) * T], -jnp.inf)
            p = jnp.exp(sm - jnp.max(sm, axis=-1, keepdims=True))
            ps.append((p * (1.0 / jnp.sum(p, axis=-1, keepdims=True))).astype(bf16))
        o = _dot(jnp.concatenate(ps, axis=0), vg)
        for n in range(4):
            g[i, :, n * HEAD:(n + 1) * HEAD] = o[n * T:(n + 1) * T].astype(bf16)

    def q_pair(k, _):
        q_dot(2 * k + 1, qb)
        q_heads(2 * k, qa)

        @pl.when(k == Q_FWD)
        def _():
            ag['x0']().wait_recv()
            ag['d0']().start()
            ag['y1']().wait_recv()
            ag['d1']().start()
            for key in ('x2', 'y3', 'x3', 'y2'):
                ag[key]().start()

        q_dot(2 * k + 2, qa)
        q_heads(2 * k + 1, qb)
        b_copy('e2', k, k).start()
        return 0

    q_dot(0, qa)
    lax.fori_loop(0, NQ // 2 - 1, q_pair, 0)
    q_dot(NQ - 1, qb)
    b_copy('e2', 3, 3).start()
    for key in ('ix', 'iy', 'id', 'x1', 'y0'):
        ag[key]().wait_recv()
    for key in ('icx', 'icy', 'icd', 'cx0', 'cy0'):
        ag[key]().start()
    q_heads(NQ - 2, qa)
    q_heads(NQ - 1, qb)

    base = ((ep * 32 + e0) * CAP).astype(f32)

    def weights(r):
        for half in range(2):
            row = lax.broadcasted_iota(jnp.int32, (T, T), 0).astype(f32) + (base + float(half * T))
            w = jnp.zeros((T, T), f32)
            d = jnp.zeros((T, T), f32)
            for j in range(TOP):
                hit = row == info[r, pl.ds(j, 1), :]
                w = jnp.where(hit, info[r, pl.ds(TOP + j, 1), :], w)
                d = jnp.where(hit, 1.0, d)
            wt = w.T
            hi = wt.astype(bf16)
            rest = wt - hi.astype(f32)
            mid = rest.astype(bf16)
            low = (rest - mid.astype(f32)).astype(bf16)
            for n, part in enumerate((hi, mid, low)):
                ws[r, pl.ds(n * T, T), half * T:(half + 1) * T] = part
            ds[r, pl.ds(half * T, T), :] = d.astype(bf16)

    def rows_of(r, k):
        rows = _dot(ds[r], u[r, k]).astype(bf16)
        x[:, pl.ds(pl.multiple_of(r * CAP, CAP), CAP), k * 512:(k + 1) * 512] = rows.reshape(EL, CAP, 512)

    def build(r, _):
        weights(r)
        for k in range(2):
            rows_of(r, k)
        return 0

    for key in ('ic', 'c0'):
        ag[key]().wait_recv()
    lax.fori_loop(0, 4, build, 0)
    for key in ('d0', 'd1'):
        ag[key]().wait_recv()
    ag['cd0']().start()
    for key in ('icx', 'icy', 'icd', 'cx0', 'cy0'):
        ag[key]().wait_recv()
    lax.fori_loop(4, 7, build, 0)
    ag['cd0']().wait_recv()
    build(7, 0)

    def first_half(e, _):
        s = lax.rem(A_EXP + e, NA)
        e_wait(s)
        for n in range(2):
            h = _dot(x[e, :, :KH], ra[s, pl.ds(n * KH, KH), :])
            for j in range(3):
                big[e * 6 + n * 3 + j] = h[:, j * HW:(j + 1) * HW]
        a_start(A_EXP + e + NA, A_EXP + NA, A_FFN)

        @pl.when(e == E_FWD[0])
        def _():
            ag['x2']().wait_recv()
            ag['d2']().start()
            ag['y3']().wait_recv()
            ag['d3']().start()

        @pl.when(e == E_FWD[1])
        def _():
            for key in ('x3', 'y2'):
                ag[key]().wait_recv()
            for key in ('cx1', 'cy1'):
                ag[key]().start()

        @pl.when(e == E_FWD[2])
        def _():
            for key in ('d2', 'd3'):
                ag[key]().wait_recv()
            ag['cd1']().start()

        @pl.when(e == EL - 9)
        def _():
            for key in ('c1', 'cx1', 'cy1', 'cd1'):
                ag[key]().wait_recv()

        @pl.when(e >= EL - 8)
        def _():
            for k in range(2, 4):
                rows_of(e - (EL - 8), k)
        return 0

    lax.fori_loop(0, EL, first_half, 0)

    def second_half(i, _):
        e = EL - 1 - i
        s = lax.rem(A_EXP + EL + i, NA)
        e_wait(s)
        hs = []
        for n in range(2):
            h = _dot(x[e, :, KH:], ra[s, pl.ds(n * KH, KH), :])
            hs.append([h[:, j * HW:(j + 1) * HW] + big[e * 6 + n * 3 + j] for j in range(3)])
        a_start(A_EXP + EL + i + NA, A_EXP + EL + NA, A_FFN + NA)
        for j in range(3):
            x[e, :, j * HW:(j + 1) * HW] = (hs[0][j] * jax.nn.sigmoid(hs[0][j]) * hs[1][j]).astype(bf16)
        return 0

    lax.fori_loop(0, EL, second_half, 0)
    pl.semaphore_signal(ready, inc=1, device_id=pc, device_id_type=MESH)

    YC = 1024

    def chunk(c):
        def part(k, _):
            t = 4 * c + k
            s = lax.rem(t, NB)
            b_copy('e2', t, s).wait()
            for i in range(4):
                x[4 * k + i, :, YC:YC + CW] = _dot(x[4 * k + i, :, :FE], rb[s, i]).astype(bf16)
            b_start(t + NB, NB, B_WO + NB)
            return 0

        if c == 0:
            lax.fori_loop(0, 4, part, 0)
            pl.semaphore_wait(ready, 1)
        else:
            lax.fori_loop(0, 2, part, 0)
            rs_first(c - 1)
            if c == 2:
                rs_second(0)
            lax.fori_loop(2, 4, part, 0)

        for q in (7, 5, 6, 4, 3, 1, 2, 0):
            r = PLACE[q]
            yr = x[:, r * CAP:(r + 1) * CAP, YC:YC + CW].reshape(2 * T, CW)
            three = _dot(ws[r], yr)
            m = (three[:T] + three[T:2 * T]) + three[2 * T:]
            big[sums(c, q, 0)] = m[:, :HW]
            big[sums(c, q, 1)] = m[:, HW:]
            if q >= 4:
                rs('c%d' % (q - 4), c).start()

    for c in range(NC):
        chunk(c)

    def wo_step(n, _):
        cols = pl.ds(pl.multiple_of(n * CW, CW), CW)
        prod = None
        for half in range(2):
            t = B_WO + 2 * n + half
            s = lax.rem(t, NB)
            b_copy('wo', 2 * n + half, s).wait()
            for i in range(4):
                term = _dot(g[half * 4 + i, :, pl.ds(0, QT)], rb[s, i, pl.ds(0, QT), :])
                prod = term if prod is None else prod + term
            b_start(t + NB, B_WO + NB, B_W2 + NB)
        ar[:, cols] = (h0[0, :, cols].astype(f32) + prod).astype(bf16)

        @pl.when(n == 0)
        def _():
            rs_first(NC - 1)
            rs_second(1)
        return 0

    lax.fori_loop(0, D // CW, wo_step, 0)

    def znorm(i, _):
        rows = pl.ds(pl.multiple_of(i * 16, 16), 16)
        xf = ar[rows, :].astype(f32)
        xr = xf * lax.rsqrt(jnp.mean(xf * xf, axis=-1, keepdims=True) + EPS)
        xz[rows, :] = (xr * nf[...].astype(f32)[None, :]).astype(bf16)
        return 0

    lax.fori_loop(0, T // 16, znorm, 0, unroll=4)

    def ffn(i, _):
        t = A_FFN + 2 * i
        s1, s3 = lax.rem(t, NA), lax.rem(t + 1, NA)
        a_copy('w1', i, s1).wait()
        h1 = _dot(xz[...], ra[s1])
        a_copy('w3', i, s3).wait()
        h3 = _dot(xz[...], ra[s3])
        for k in (0, 1):
            a_start(t + NA + k, A_FFN + NA, A_END)
        g[i] = (h1 * jax.nn.sigmoid(h1) * h3).astype(bf16)
        for at, c in ((1, 2), (5, 3)):
            @pl.when(i == at)
            def _():
                rs_second(c)
        return 0

    lax.fori_loop(0, NF, ffn, 0)

    for n in range(D // CW):
        cols = slice(n * CW, (n + 1) * CW)
        prod = None
        for half in range(2):
            t = B_W2 + 2 * n + half
            s = t % NB
            b_copy('w2', 2 * n + half, s).wait()
            for i in range(4):
                term = _dot(g[half * 4 + i], rb[s, i])
                prod = term if prod is None else prod + term
            if t + NB < B_END:
                b_copy('w2', 2 * n + half + NB, s).start()
        rs_last(n, ar[:, cols].astype(f32) + prod)

    for key in ag:
        ag[key]().wait_send()
    for c in range(NC):
        for name in ('c0', 'c1', 'c2', 'c3', 'xa', 'xb', 'ya', 'yb', 'y2', 'x2'):
            rs(name, c).wait_send()


def solution(mesh):
    ang = (np.arange(T, dtype=np.float32)[:, None]
           * (ROPE_BASE ** (-2.0 * np.arange(HEAD // 2) / HEAD)).astype(np.float32)[None, :])
    cos = np.cos(ang.astype(np.float64)).astype(np.float32)
    sin = np.sin(ang.astype(np.float64)).astype(np.float32)
    cos2 = np.concatenate([cos, cos], axis=1)
    sin2 = np.concatenate([-sin, sin], axis=1)
    ncopies = 27 + 10 * NC

    def local(h0, idx, slot, na, wq, wk, wv, wo, nf, w1, w3, w2, nm, wr, ue1, ue3, ue2):
        vm = pl.BlockSpec(memory_space=pltpu.VMEM)
        hb = pl.BlockSpec(memory_space=pl.ANY)
        return pl.pallas_call(
            _kernel,
            out_shape=jax.ShapeDtypeStruct(h0.shape, bf16),
            in_specs=[vm] * 9 + [hb] * 10,
            out_specs=vm,
            scratch_shapes=[
                pltpu.VMEM((T, D), bf16),
                pltpu.VMEM((T, D), bf16),
                pltpu.VMEM((T, QT), f32),
                pltpu.VMEM((T, QT), f32),
                pltpu.VMEM((8, 4, T, D // 4), bf16),
                pltpu.VMEM((8, 2 * TOP, T), f32),
                pltpu.VMEM((8, 3 * T, 2 * T), bf16),
                pltpu.VMEM((8, 2 * T, T), bf16),
                pltpu.VMEM((EL, T, D), bf16),
                pltpu.VMEM((4, T, HEAD), bf16),
                pltpu.VMEM((4, T, HEAD), bf16),
                pltpu.VMEM((NF, T, FE), bf16),
                pltpu.VMEM((NBLK, T, HW), f32),
                pltpu.VMEM((NA, D, FE), bf16),
                pltpu.VMEM((NB, 4, FE, CW), bf16),
                pltpu.SemaphoreType.DMA((NA,)),
                pltpu.SemaphoreType.DMA((NB,)),
                pltpu.SemaphoreType.DMA((ncopies,)),
                pltpu.SemaphoreType.DMA((ncopies,)),
                pltpu.SemaphoreType.REGULAR,
            ],
            compiler_params=pltpu.CompilerParams(collective_id=0, has_side_effects=True,
                                                 vmem_limit_bytes=67043328),
            name='scmoe',
        )(h0, jnp.swapaxes(idx, 1, 2), jnp.swapaxes(slot, 1, 2), na, nf, nm,
          jnp.asarray(cos2), jnp.asarray(sin2), wr, wq, wk, wv, wo.reshape(8, QT, D),
          w1, w3, w2.reshape(8, FE, D), ue1, ue3, ue2)

    rows = P(('dp', 'ep'))
    in_specs = (rows,) * 3 + (P(),) * 11 + (P('ep'),) * 3
    return jax.shard_map(local, mesh=mesh, in_specs=in_specs, out_specs=rows, check_vma=False)
```

time: 102 us -> 94.5 us (0.926)
  Pallas kernels: 99.9 us -> 92.4 us
    pallas_call x1, Pallas kernels: 99.9 us -> 92.4 us  [local(): pl.pallas_call(_kernel, out_shape=jax.ShapeDtypeStruct(h0.shape, bf16), i...]
where the time goes in v3:
time: 94.5 us; the launch traced here: 94.3 us
  Pallas kernels  92.4 us (98%)
  local copies, waits for them, and re-layouts  1.88 us (2%)
    pallas_call x1, Pallas kernels, local(): pl.pallas_call(_kernel, out_shape=jax.ShapeDtypeStruct(h0.shape, bf16), i...  92.4 us

profile of v3, /device:TPU:0, one launch (start us, length us, event | category | flops | bytes accessed | tf_op | source)
XLA Modules:
  0.0 94.3 jit_solution(14086553754215124347)
XLA Ops:
  0.0 92.4 %scmoe.1 = bf16[1,128,2048]{2,1,0:T(8,128)(2,1)} custom-call(bf16[1,128,2048]{2,1,0:T(8,128)(2,1)} %h0.1, s32[1,8,128]{2,1,0:T(8,128)} %bitcast.6, s32[1,8,128]{2,1,0:T(8,128)} %bitcast.7, bf16[2048]{0:T(1024)(128)(2,1)} %na.1, bf16[2048]{0:T(1024)(128)(2,1)} %nf.1, bf16[2048]{0:T(1024)(128)(2,1)} %nm.1, f32[128,128]{1,0:T(8,128)} %constant.4.clone.cos, ...), custom_call_target="tpu_custom_call" | custom-call | tf_op jit(solution)/shard_map/scmoe/pallas_call | solution.py:530
  92.4 1.9 %copy.21 = bf16[1,128,2048]{2,1,0:T(8,128)(2,1)} copy(bf16[1,128,2048]{2,1,0:T(8,128)(2,1)} %scmoe.1) | data formatting | bytes 1048576

commit v4 on v3

v4 whole, which is shorter than its diff:
```python
import functools

import jax
import jax.numpy as jnp
import numpy as np
from jax import lax
from jax.experimental import pallas as pl
from jax.experimental.pallas import tpu as pltpu
from jax.sharding import PartitionSpec as P

MESH = pl.DeviceIdType.MESH
HEAD = 128
EPS = 1e-6
ROPE_BASE = 10000.0

T, D, FE, FF, TOP, CAP = 128, 2048, 768, 6144, 8, 16
EL = 16
QT = 512
CW = 512
NC = D // CW
HW = CW // 2
NS = 8
E2 = 2 * FE
KH = D // 2
NQ = 8
Q_FWD = 1
E_FWD = (0, 2, 4)
EARLY = 6
PLACE = (0, 2, 3, 6, 1, 4, 5, 7)
NF = FF // FE
T_Q = 2
T_EXP = T_Q + NQ
T_E2 = T_EXP + 2 * EL
T_WO = T_E2 + 8 * NC
T_FFN = T_WO + 2 * NC
T_W2 = T_FFN + 2 * NF
T_END = T_W2 + 3 * NC
RC = 16 * NC
R1 = RC + 8 * NC
R2 = R1 + 4 * NC
NBLK = R2 + 2 * NC

f32, bf16 = jnp.float32, jnp.bfloat16


def _dot(a, b):
    return jnp.dot(a, b, preferred_element_type=f32)


def _mult(v):
    return v if isinstance(v, int) else pl.multiple_of(v, 256)


def _kernel(h0, idx, slot, na, nf, nm, cos, sin, wr, wq, wk, wv, wo, w1, w3, w2, ue1, ue3, ue2, out,
            xz, ar, fs, qa, qb, u, info, ws, ds, x, kk, vv, g, big, ring,
            sem, send, recv, ready):
    dp, ep = lax.axis_index('dp'), lax.axis_index('ep')
    px = (dp, lax.rem(ep + 2, 4))
    py = (1 - dp, ep)
    pc = (dp, ep + 1 - 2 * lax.rem(ep, 2))
    e0 = dp * EL

    def start(t, lo=0, hi=T_END, par=None):
        s = t % NS

        def tile(src, rows=2048, at=0, width=CW):
            pltpu.make_async_copy(src, ring.at[s, pl.ds(at, rows), pl.ds(0, width)], sem.at[s]).start()

        def q(k):
            tile(wq.at[:, pl.ds(_mult(k * QT), QT)])

        def experts(k):
            first = k < EL
            e = e0 + jnp.where(first, k, 2 * EL - 1 - k)
            rows = pl.ds(_mult(jnp.where(first, 0, KH)), KH)
            tile(ue1.at[e, rows, :], KH, 0, FE)
            tile(ue3.at[e, rows, :], KH, KH, FE)

        def e2(k):
            tile(ue2.at[pl.ds(_mult(e0 * FE + k % 8 * E2), E2), pl.ds(_mult(k // 8 * CW), CW)], E2)

        def out_proj(k):
            tile(wo.at[pl.ds(_mult(k % 2 * 2048), 2048), pl.ds(_mult(k // 2 * CW), CW)])

        def up(k):
            tile(w1.at[:, pl.ds(_mult(k // 2 * FE), FE)], width=FE)

        def gate(k):
            tile(w3.at[:, pl.ds(_mult(k // 2 * FE), FE)], width=FE)

        def down(k):
            tile(w2.at[pl.ds(_mult(k % 3 * 2048), 2048), pl.ds(_mult(k // 3 * CW), CW)])

        for first, last, fns in ((T_Q, T_EXP, (q,)), (T_EXP, T_E2, (experts,)), (T_E2, T_WO, (e2,)),
                                 (T_WO, T_FFN, (out_proj,)), (T_FFN, T_W2, (up, gate)), (T_W2, T_END, (down,))):
            a, b = max(first, lo), min(last, hi)
            if a >= b:
                continue
            for p, fn in enumerate(fns):
                if isinstance(t, int):
                    if a <= t < b and (t - first) % len(fns) == p:
                        fn(t - first)
                elif (a, b) == (lo, hi) and (len(fns) == 1 or par is not None):
                    if len(fns) == 1 or p == par:
                        fn(t - first)
                else:
                    cond = (t >= a) & (t < b)
                    if len(fns) > 1:
                        cond = cond & ((t - first) % len(fns) == p)

                    @pl.when(cond)
                    def _():
                        fn(t - first)

    def wait(t, rows=2048, width=CW):
        s = t % NS
        pltpu.make_async_copy(w1.at[pl.ds(0, rows), pl.ds(0, width)], ring.at[s, pl.ds(0, rows), pl.ds(0, width)],
                              sem.at[s]).wait()
        return s

    specs = {}

    def rdma(key, src, dst, to):
        i = specs.setdefault(key, len(specs))
        return pltpu.make_async_remote_copy(src_ref=src, dst_ref=dst, send_sem=send.at[i], recv_sem=recv.at[i],
                                            device_id=to, device_id_type=MESH)

    ag = {
        'ix': lambda: rdma('ix', info.at[0], info.at[2], px),
        'iy': lambda: rdma('iy', info.at[0], info.at[3], py),
        'id': lambda: rdma('id', info.at[2], info.at[6], py),
        'ic': lambda: rdma('ic', info.at[0], info.at[1], pc),
        'c0': lambda: rdma('c0', u.at[0, pl.ds(0, 2)], u.at[1, pl.ds(0, 2)], pc),
        'c1': lambda: rdma('c1', u.at[0, pl.ds(2, 2)], u.at[1, pl.ds(2, 2)], pc),
        'x0': lambda: rdma('x0', u.at[0, 0], u.at[2, 0], px),
        'y0': lambda: rdma('y0', u.at[0, 0], u.at[3, 0], py),
        'x1': lambda: rdma('x1', u.at[0, 1], u.at[2, 1], px),
        'y1': lambda: rdma('y1', u.at[0, 1], u.at[3, 1], py),
        'x2': lambda: rdma('x2', u.at[0, 2], u.at[2, 2], px),
        'y2': lambda: rdma('y2', u.at[0, 2], u.at[3, 2], py),
        'x3': lambda: rdma('x3', u.at[0, 3], u.at[2, 3], px),
        'y3': lambda: rdma('y3', u.at[0, 3], u.at[3, 3], py),
        'd0': lambda: rdma('d0', u.at[2, 0], u.at[6, 0], py),
        'd1': lambda: rdma('d1', u.at[3, 1], u.at[6, 1], px),
        'd2': lambda: rdma('d2', u.at[2, 2], u.at[6, 2], py),
        'd3': lambda: rdma('d3', u.at[3, 3], u.at[6, 3], px),
        'cx0': lambda: rdma('cx0', u.at[2, pl.ds(0, 2)], u.at[4, pl.ds(0, 2)], pc),
        'cx1': lambda: rdma('cx1', u.at[2, pl.ds(2, 2)], u.at[4, pl.ds(2, 2)], pc),
        'cy0': lambda: rdma('cy0', u.at[3, pl.ds(0, 2)], u.at[5, pl.ds(0, 2)], pc),
        'cy1': lambda: rdma('cy1', u.at[3, pl.ds(2, 2)], u.at[5, pl.ds(2, 2)], pc),
        'cd0': lambda: rdma('cd0', u.at[6, pl.ds(0, 2)], u.at[7, pl.ds(0, 2)], pc),
        'cd1': lambda: rdma('cd1', u.at[6, pl.ds(2, 2)], u.at[7, pl.ds(2, 2)], pc),
        'icx': lambda: rdma('icx', info.at[2], info.at[4], pc),
        'icy': lambda: rdma('icy', info.at[3], info.at[5], pc),
        'icd': lambda: rdma('icd', info.at[6], info.at[7], pc),
    }
    for key in ag:
        specs.setdefault(key, len(specs))

    def sums(c, q, half=0):
        return c * 16 + q * 2 + half

    def rs(name, c):
        key = (name, c)
        if name[0] == 'c':
            n = int(name[1])
            return rdma(key, big.at[pl.ds(sums(c, 4 + n), 2)], big.at[pl.ds(RC + c * 8 + n * 2, 2)], pc)
        src, dst, to = {
            'xa': (sums(c, 1, 0), R1 + c * 4, px),
            'xb': (sums(c, 3, 0), R1 + c * 4 + 1, px),
            'ya': (sums(c, 2, 1), R1 + c * 4 + 2, py),
            'yb': (sums(c, 3, 1), R1 + c * 4 + 3, py),
            'y2': (sums(c, 2, 0), R2 + c * 2, py),
            'x2': (sums(c, 1, 1), R2 + c * 2 + 1, px),
        }[name]
        return rdma(key, big.at[src], big.at[dst], to)

    def rs_first(c, qs):
        for q in qs:
            rs('c%d' % q, c).wait_recv()
            for half in range(2):
                k = sums(c, q, half)
                big[k] = big[k] + big[RC + c * 8 + q * 2 + half]
            for name in ((), ('xa',), ('ya',), ('xb', 'yb'))[q]:
                rs(name, c).start()

    def rs_second(c):
        rs('xb', c).wait_recv()
        big[sums(c, 2, 0)] = big[sums(c, 2, 0)] + big[R1 + c * 4 + 1]
        rs('y2', c).start()
        rs('yb', c).wait_recv()
        big[sums(c, 1, 1)] = big[sums(c, 1, 1)] + big[R1 + c * 4 + 3]
        rs('x2', c).start()

    def rs_last(c, f):
        rs('xa', c).wait_recv()
        rs('y2', c).wait_recv()
        m = (big[sums(c, 0, 0)] + big[R1 + c * 4]) + big[R2 + c * 2]
        out[0, :, c * CW:c * CW + HW] = (f[:, :HW] + m).astype(bf16)
        rs('ya', c).wait_recv()
        rs('x2', c).wait_recv()
        m = (big[sums(c, 0, 1)] + big[R1 + c * 4 + 2]) + big[R2 + c * 2 + 1]
        out[0, :, c * CW + HW:(c + 1) * CW] = (f[:, HW:] + m).astype(bf16)

    barrier = pltpu.get_barrier_semaphore()
    for to in (px, py, pc):
        pl.semaphore_signal(barrier, inc=1, device_id=to, device_id_type=MESH)
    for i, src in enumerate((wk, wv)):
        pltpu.make_async_copy(src, ring.at[i, :, pl.ds(0, QT)], sem.at[i]).start()
    for t in range(T_Q, NS):
        start(t, T_Q, NS)

    def norms(i, _):
        rows = pl.ds(pl.multiple_of(i * 16, 16), 16)
        xf = h0[0, rows, :].astype(f32)
        xr = xf * lax.rsqrt(jnp.mean(xf * xf, axis=-1, keepdims=True) + EPS)
        un = (xr * nm[...].astype(f32)[None, :]).astype(bf16)
        for k in range(4):
            u[0, k, rows, :] = un[:, k * 512:(k + 1) * 512]
        xz[rows, :] = (xr * na[...].astype(f32)[None, :]).astype(bf16)
        return 0

    lax.fori_loop(0, T // 16, norms, 0, unroll=4)
    pl.semaphore_wait(barrier, 3)
    for key in ('x0', 'y1', 'c0'):
        ag[key]().start()

    logits = _dot(u[0, 0], wr[pl.ds(0, 512), :])
    for k in range(1, 4):
        logits = logits + _dot(u[0, k], wr[pl.ds(k * 512, 512), :])
    lt = logits.T
    idt = idx[0].astype(f32)
    slt = slot[0].astype(f32)
    ex = lax.broadcasted_iota(jnp.int32, (T, T), 0).astype(f32)
    sel = jnp.concatenate(
        [jnp.sum(jnp.where(ex == idt[j:j + 1, :], lt, 0.0), axis=0, keepdims=True) for j in range(TOP)], axis=0)
    gate = jnp.exp(sel - jnp.max(sel, axis=0, keepdims=True))
    gate = gate / jnp.sum(gate, axis=0, keepdims=True)
    info[0, pl.ds(0, TOP), :] = idt * float(CAP) + slt
    info[0, pl.ds(TOP, TOP), :] = gate
    for key in ('ix', 'iy', 'ic', 'x1', 'y0', 'c1'):
        ag[key]().start()

    cs, sn = cos[...], sin[...]

    def rope(v):
        return (v * cs + pltpu.roll(v, HEAD // 2, 1) * sn).astype(bf16)

    wait(0)
    wait(1)
    kf = _dot(xz[...], ring[0, :, pl.ds(0, QT)])
    vf = _dot(xz[...], ring[1, :, pl.ds(0, QT)])
    for n in range(4):
        kk[n] = rope(kf[:, n * HEAD:(n + 1) * HEAD])
        vv[n] = vf[:, n * HEAD:(n + 1) * HEAD].astype(bf16)
    start(NS, T_Q, T_E2)
    start(NS + 1, T_Q, T_E2)
    causal = lax.broadcasted_iota(jnp.int32, (T, T), 0) >= lax.broadcasted_iota(jnp.int32, (T, T), 1)

    def q_dot(s, dst):
        dst[...] = _dot(xz[...], ring[s, :, pl.ds(0, QT)])

    def q_heads(i, src):
        kg, vg = kk[i // 2], vv[i // 2]
        qs = jnp.concatenate([rope(src[:, n * HEAD:(n + 1) * HEAD]) for n in range(4)], axis=0)
        sc = lax.dot_general(qs, kg, (((1,), (1,)), ((), ())), preferred_element_type=f32) * HEAD ** -0.5
        ps = []
        for n in range(4):
            sm = jnp.where(causal, sc[n * T:(n + 1) * T], -jnp.inf)
            p = jnp.exp(sm - jnp.max(sm, axis=-1, keepdims=True))
            ps.append((p * (1.0 / jnp.sum(p, axis=-1, keepdims=True))).astype(bf16))
        o = _dot(jnp.concatenate(ps, axis=0), vg)
        for n in range(4):
            g[:, pl.ds(_mult(i * QT) + n * HEAD, HEAD)] = o[n * T:(n + 1) * T].astype(bf16)

    def q_pair(k, _):
        t = T_Q + 2 * k + 1
        s = wait(t), wait(t + 1)
        q_dot(s[0], qb)
        start(t + NS, T_EXP, T_E2)
        q_heads(2 * k, qa)
        q_dot(s[1], qa)
        start(t + 1 + NS, T_EXP, T_E2)
        q_heads(2 * k + 1, qb)

        @pl.when(k == Q_FWD)
        def _():
            ag['ix']().wait_recv()
            ag['id']().start()
            ag['x0']().wait_recv()
            ag['d0']().start()
            ag['y1']().wait_recv()
            ag['d1']().start()
            for key in ('x2', 'y3', 'x3', 'y2'):
                ag[key]().start()

        return 0

    q_dot(wait(T_Q), qa)
    start(T_Q + NS, T_EXP, T_E2)
    lax.fori_loop(0, NQ // 2 - 1, q_pair, 0)
    s_last = wait(T_EXP - 1)
    q_dot(s_last, qb)
    q_heads(NQ - 2, qa)
    q_heads(NQ - 1, qb)
    start(T_EXP - 1 + NS, T_EXP, T_E2)
    for key in ('iy', 'id', 'x1', 'y0'):
        ag[key]().wait_recv()
    for key in ('icx', 'icy', 'icd', 'cx0', 'cy0'):
        ag[key]().start()

    base = ((ep * 32 + e0) * CAP).astype(f32)

    def weights(r):
        for half in range(2):
            row = lax.broadcasted_iota(jnp.int32, (T, T), 0).astype(f32) + (base + float(half * T))
            w = jnp.zeros((T, T), f32)
            d = jnp.zeros((T, T), f32)
            for j in range(TOP):
                hit = row == info[r, pl.ds(j, 1), :]
                w = jnp.where(hit, info[r, pl.ds(TOP + j, 1), :], w)
                d = jnp.where(hit, 1.0, d)
            wt = w.T
            hi = wt.astype(bf16)
            rest = wt - hi.astype(f32)
            mid = rest.astype(bf16)
            low = (rest - mid.astype(f32)).astype(bf16)
            for n, part in enumerate((hi, mid, low)):
                ws[r, pl.ds(n * T, T), half * T:(half + 1) * T] = part
            ds[r, pl.ds(half * T, T), :] = d.astype(bf16)

    def rows_of(r, k):
        rows = _dot(ds[r], u[r, k]).astype(bf16)
        x[:, pl.ds(pl.multiple_of(r * CAP, CAP), CAP), k * 512:(k + 1) * 512] = rows.reshape(EL, CAP, 512)

    def build(r, _):
        weights(r)
        for k in range(2):
            rows_of(r, k)
        return 0

    for key in ('ic', 'c0'):
        ag[key]().wait_recv()
    lax.fori_loop(0, 4, build, 0)
    for key in ('d0', 'd1'):
        ag[key]().wait_recv()
    ag['cd0']().start()
    for key in ('icx', 'icy', 'icd', 'cx0', 'cy0'):
        ag[key]().wait_recv()
    lax.fori_loop(4, 7, build, 0)
    ag['cd0']().wait_recv()
    build(7, 0)

    def products(lhs, s):
        ha = _dot(lhs, ring[s, pl.ds(0, KH), :])
        hc = _dot(lhs, ring[s, pl.ds(KH, KH), :])
        return [h[:, j * HW:(j + 1) * HW] for h in (ha, hc) for j in range(3)]

    def first_half(i, _):
        t = T_EXP + 2 * i
        slots = [wait(t + k, width=FE) for k in range(2)]
        for k in range(2):
            e = 2 * i + k
            for j, h in enumerate(products(x[e, :, :KH], slots[k])):
                big[e * 6 + j] = h
            start(t + k + NS, T_EXP + NS, T_E2)

    def first_early(i, _):
        first_half(i, 0)

        @pl.when(i == E_FWD[0])
        def _():
            ag['x2']().wait_recv()
            ag['d2']().start()
            ag['y3']().wait_recv()
            ag['d3']().start()

        @pl.when(i == E_FWD[1])
        def _():
            for key in ('x3', 'y2'):
                ag[key]().wait_recv()
            for key in ('cx1', 'cy1'):
                ag[key]().start()

        @pl.when(i == E_FWD[2])
        def _():
            for key in ('d2', 'd3'):
                ag[key]().wait_recv()
            ag['cd1']().start()
        return 0

    def first_late(i, _):
        first_half(i, 0)
        for k in range(2, 4):
            for j in range(4):
                rows_of(4 * (i - EARLY) + j, k)
        return 0

    lax.fori_loop(0, EARLY, first_early, 0)
    for key in ('c1', 'cx1', 'cy1', 'cd1'):
        ag[key]().wait_recv()
    lax.fori_loop(EARLY, 8, first_late, 0)

    def second_half(lo, hi):
        def step(i, _):
            t = T_EXP + EL + 2 * i
            slots = [wait(t + k, width=FE) for k in range(2)]
            for k in range(2):
                e = EL - 1 - (2 * i + k)
                hs = [h + big[e * 6 + j] for j, h in enumerate(products(x[e, :, KH:], slots[k]))]
                start(t + k + NS, lo, hi)
                for j in range(3):
                    x[e, :, j * HW:(j + 1) * HW] = (hs[j] * jax.nn.sigmoid(hs[j]) * hs[3 + j]).astype(bf16)
            return 0
        return step

    turn = (EL - NS) // 2
    lax.fori_loop(0, turn, second_half(T_EXP + EL + NS, T_E2), 0)
    if (EL - NS) % 2:
        second_half(0, T_END)(turn, 0)
        turn += 1
    lax.fori_loop(turn, EL // 2, second_half(T_E2, T_WO), 0)
    pl.semaphore_signal(ready, inc=1, device_id=pc, device_id_type=MESH)

    YC = 1024

    def chunk(c):
        def part(k):
            t = T_E2 + 8 * c + 4 * k
            slots = [wait(t + j, E2) for j in range(4)]
            for j in range(4):
                for i in range(2):
                    e = 8 * k + 2 * j + i
                    x[e, :, YC:YC + CW] = _dot(x[e, :, :FE], ring[slots[j], pl.ds(i * FE, FE), pl.ds(0, CW)]).astype(bf16)
                start(t + j + NS)

        part(0)
        if c > 0:
            rs_first(c - 1, (1, 2, 0))
        part(1)
        if c == 0:
            pl.semaphore_wait(ready, 1)
        if c == 2:
            rs_second(0)

        for q in (7, 5, 6, 4, 3, 1, 2, 0):
            r = PLACE[q]
            yr = x[:, r * CAP:(r + 1) * CAP, YC:YC + CW].reshape(2 * T, CW)
            three = _dot(ws[r], yr)
            m = (three[:T] + three[T:2 * T]) + three[2 * T:]
            big[sums(c, q, 0)] = m[:, :HW]
            big[sums(c, q, 1)] = m[:, HW:]
            if q >= 4:
                rs('c%d' % (q - 4), c).start()
        rs_first(c, (3,))

    for c in range(NC):
        chunk(c)

    for n in range(D // CW):
        cols = slice(n * CW, (n + 1) * CW)
        t = T_WO + 2 * n
        s0, s1 = wait(t), wait(t + 1)
        prod = _dot(g[:, :2048], ring[s0, :, pl.ds(0, CW)])
        start(t + NS)
        prod = prod + _dot(g[:, 2048:4096], ring[s1, :, pl.ds(0, CW)])
        start(t + 1 + NS)
        ar[:, cols] = (h0[0, :, cols].astype(f32) + prod).astype(bf16)
        if n == 0:
            rs_first(NC - 1, (1, 2, 0))
            rs_second(1)

    def znorm(i, _):
        rows = pl.ds(pl.multiple_of(i * 16, 16), 16)
        xf = ar[rows, :].astype(f32)
        xr = xf * lax.rsqrt(jnp.mean(xf * xf, axis=-1, keepdims=True) + EPS)
        xz[rows, :] = (xr * nf[...].astype(f32)[None, :]).astype(bf16)
        return 0

    lax.fori_loop(0, T // 16, znorm, 0, unroll=4)

    def ffn(lo, hi):
        def step(i, _):
            t = T_FFN + 4 * i
            slots = [wait(t + k, width=FE) for k in range(4)]
            for k in range(2):
                h1 = _dot(xz[...], ring[slots[2 * k]])
                start(t + 2 * k + NS, lo, hi, NS % 2)
                h3 = _dot(xz[...], ring[slots[2 * k + 1]])
                start(t + 2 * k + 1 + NS, lo, hi, (NS + 1) % 2)
                g[:, pl.ds(_mult(i * 2 * FE) + k * FE, FE)] = (h1 * jax.nn.sigmoid(h1) * h3).astype(bf16)
            return 0
        return step

    turn = (2 * NF - NS) // 4
    lax.fori_loop(0, turn, ffn(T_FFN + NS, T_W2), 0)
    rs_second(2)
    if (2 * NF - NS) % 4:
        ffn(0, T_END)(turn, 0)
        turn += 1
    lax.fori_loop(turn, NF // 2, ffn(T_W2, T_END), 0)
    rs_second(3)

    for n in range(D // CW):
        cols = slice(n * CW, (n + 1) * CW)
        t = T_W2 + 3 * n
        slots = [wait(t + k) for k in range(3)]
        prod = None
        for k in range(3):
            term = _dot(g[:, k * 2048:(k + 1) * 2048], ring[slots[k], :, pl.ds(0, CW)])
            prod = term if prod is None else prod + term
            start(t + k + NS, T_W2, T_END)
        if n == 0:
            fs[...] = ar[:, cols].astype(f32) + prod
            continue
        if n == 1:
            rs_last(0, fs[...])
        rs_last(n, ar[:, cols].astype(f32) + prod)

    for key in ag:
        ag[key]().wait_send()
    for c in range(NC):
        for name in ('c0', 'c1', 'c2', 'c3', 'xa', 'xb', 'ya', 'yb', 'y2', 'x2'):
            rs(name, c).wait_send()


def solution(mesh):
    ang = (np.arange(T, dtype=np.float32)[:, None]
           * (ROPE_BASE ** (-2.0 * np.arange(HEAD // 2) / HEAD)).astype(np.float32)[None, :])
    cos = np.cos(ang.astype(np.float64)).astype(np.float32)
    sin = np.sin(ang.astype(np.float64)).astype(np.float32)
    cos2 = np.concatenate([cos, cos], axis=1)
    sin2 = np.concatenate([-sin, sin], axis=1)
    ncopies = 27 + 10 * NC

    def local(h0, idx, slot, na, wq, wk, wv, wo, nf, w1, w3, w2, nm, wr, ue1, ue3, ue2):
        vm = pl.BlockSpec(memory_space=pltpu.VMEM)
        hb = pl.BlockSpec(memory_space=pl.ANY)
        return pl.pallas_call(
            _kernel,
            out_shape=jax.ShapeDtypeStruct(h0.shape, bf16),
            in_specs=[vm] * 9 + [hb] * 10,
            out_specs=vm,
            scratch_shapes=[
                pltpu.VMEM((T, D), bf16),
                pltpu.VMEM((T, D), bf16),
                pltpu.VMEM((T, CW), f32),
                pltpu.VMEM((T, QT), f32),
                pltpu.VMEM((T, QT), f32),
                pltpu.VMEM((8, 4, T, D // 4), bf16),
                pltpu.VMEM((8, 2 * TOP, T), f32),
                pltpu.VMEM((8, 3 * T, 2 * T), bf16),
                pltpu.VMEM((8, 2 * T, T), bf16),
                pltpu.VMEM((EL, T, D), bf16),
                pltpu.VMEM((4, T, HEAD), bf16),
                pltpu.VMEM((4, T, HEAD), bf16),
                pltpu.VMEM((T, FF), bf16),
                pltpu.VMEM((NBLK, T, HW), f32),
                pltpu.VMEM((NS, 2048, FE), bf16),
                pltpu.SemaphoreType.DMA((NS,)),
                pltpu.SemaphoreType.DMA((ncopies,)),
                pltpu.SemaphoreType.DMA((ncopies,)),
                pltpu.SemaphoreType.REGULAR,
            ],
            compiler_params=pltpu.CompilerParams(collective_id=0, has_side_effects=True,
                                                 vmem_limit_bytes=67043328),
            name='scmoe',
        )(h0, jnp.swapaxes(idx, 1, 2), jnp.swapaxes(slot, 1, 2), na, nf, nm,
          jnp.asarray(cos2), jnp.asarray(sin2), wr, wq, wk, wv, wo, w1, w3, w2, ue1, ue3, ue2.reshape(-1, D))

    rows = P(('dp', 'ep'))
    in_specs = (rows,) * 3 + (P(),) * 11 + (P('ep'),) * 3
    return jax.shard_map(local, mesh=mesh, in_specs=in_specs, out_specs=rows, check_vma=False)
```

time: 94.5 us -> 88.5 us (0.937)
  Pallas kernels: 92.4 us -> 86.5 us
    pallas_call x1, Pallas kernels: 92.4 us -> 86.5 us  [local(): pl.pallas_call(_kernel, out_shape=jax.ShapeDtypeStruct(h0.shape, bf16), i...]
where the time goes in v4:
time: 88.5 us; the launch traced here: 88.3 us
  Pallas kernels  86.5 us (98%)
  local copies, waits for them, and re-layouts  1.88 us (2%)
    pallas_call x1, Pallas kernels, local(): pl.pallas_call(_kernel, out_shape=jax.ShapeDtypeStruct(h0.shape, bf16), i...  86.5 us
    unnamed x1, local copies, waits for them, and re-layouts  1.88 us

profile of v4, /device:TPU:0, one launch (start us, length us, event | category | flops | bytes accessed | tf_op | source)
XLA Modules:
  0.0 88.3 jit_solution(11146600345439422713)
XLA Ops:
  0.0 86.5 %scmoe.1 = bf16[1,128,2048]{2,1,0:T(8,128)(2,1)} custom-call(bf16[1,128,2048]{2,1,0:T(8,128)(2,1)} %h0.1, s32[1,8,128]{2,1,0:T(8,128)} %bitcast.3, s32[1,8,128]{2,1,0:T(8,128)} %bitcast.4, bf16[2048]{0:T(1024)(128)(2,1)} %na.1, bf16[2048]{0:T(1024)(128)(2,1)} %nf.1, bf16[2048]{0:T(1024)(128)(2,1)} %nm.1, f32[128,128]{1,0:T(8,128)} %constant.4.clone.cos, ...), custom_call_target="tpu_custom_call" | custom-call | tf_op jit(solution)/shard_map/scmoe/pallas_call | solution.py:539
  86.5 1.9 %copy.21 = bf16[1,128,2048]{2,1,0:T(8,128)(2,1)} copy(bf16[1,128,2048]{2,1,0:T(8,128)(2,1)} %scmoe.1) | data formatting | bytes 1048576

commit v5 on v4

--- a/solution.py
+++ b/solution.py
@@ -23,16 +23,18 @@
 E2 = 2 * FE
 KH = D // 2
 NQ = 8
+NW = 1
 Q_FWD = 1
 E_FWD = (0, 2, 4)
 EARLY = 6
 PLACE = (0, 2, 3, 6, 1, 4, 5, 7)
 NF = FF // FE
 T_Q = 2
-T_EXP = T_Q + NQ
+T_WO1 = T_Q + NQ
+T_EXP = T_WO1 + 2 * NW
 T_E2 = T_EXP + 2 * EL
 T_WO = T_E2 + 8 * NC
-T_FFN = T_WO + 2 * NC
+T_FFN = T_WO + 2 * (NC - NW)
 T_W2 = T_FFN + 2 * NF
 T_END = T_W2 + 3 * NC
 RC = 16 * NC
@@ -51,8 +53,8 @@
     return v if isinstance(v, int) else pl.multiple_of(v, 256)
 
 
-def _kernel(h0, idx, slot, na, nf, nm, cos, sin, wr, wq, wk, wv, wo, w1, w3, w2, ue1, ue3, ue2, out,
-            xz, ar, fs, qa, qb, u, info, ws, ds, x, kk, vv, g, big, ring,
+def _kernel(h0_h, idx_h, slot_h, na_h, nf_h, nm_h, cos_h, sin_h, wr_h, wq, wk, wv, wo, w1, w3, w2, ue1, ue3, ue2, out,
+            h0, idx, slot, na, nf, nm, cos, sin, wr, sem_in, sem_out, xz, ar, fs, qa, qb, u, info, ws, ds, x, kk, vv, g, big, ring,
             sem, send, recv, ready):
     dp, ep = lax.axis_index('dp'), lax.axis_index('ep')
     px = (dp, lax.rem(ep + 2, 4))
@@ -82,6 +84,9 @@
         def out_proj(k):
             tile(wo.at[pl.ds(_mult(k % 2 * 2048), 2048), pl.ds(_mult(k // 2 * CW), CW)])
 
+        def out_rest(k):
+            out_proj(k + 2 * NW)
+
         def up(k):
             tile(w1.at[:, pl.ds(_mult(k // 2 * FE), FE)], width=FE)
 
@@ -91,8 +96,8 @@
         def down(k):
             tile(w2.at[pl.ds(_mult(k % 3 * 2048), 2048), pl.ds(_mult(k // 3 * CW), CW)])
 
-        for first, last, fns in ((T_Q, T_EXP, (q,)), (T_EXP, T_E2, (experts,)), (T_E2, T_WO, (e2,)),
-                                 (T_WO, T_FFN, (out_proj,)), (T_FFN, T_W2, (up, gate)), (T_W2, T_END, (down,))):
+        for first, last, fns in ((T_Q, T_WO1, (q,)), (T_WO1, T_EXP, (out_proj,)), (T_EXP, T_E2, (experts,)),
+                                 (T_E2, T_WO, (e2,)), (T_WO, T_FFN, (out_rest,)), (T_FFN, T_W2, (up, gate)), (T_W2, T_END, (down,))):
             a, b = max(first, lo), min(last, hi)
             if a >= b:
                 continue
@@ -192,23 +197,36 @@
         big[sums(c, 1, 1)] = big[sums(c, 1, 1)] + big[R1 + c * 4 + 3]
         rs('x2', c).start()
 
+    def result(c):
+        cols = pl.ds(c * CW, CW)
+        return pltpu.make_async_copy(xz.at[:, cols], out.at[0, :, cols], sem_out.at[c])
+
     def rs_last(c, f):
         rs('xa', c).wait_recv()
         rs('y2', c).wait_recv()
         m = (big[sums(c, 0, 0)] + big[R1 + c * 4]) + big[R2 + c * 2]
-        out[0, :, c * CW:c * CW + HW] = (f[:, :HW] + m).astype(bf16)
+        xz[:, c * CW:c * CW + HW] = (f[:, :HW] + m).astype(bf16)
         rs('ya', c).wait_recv()
         rs('x2', c).wait_recv()
         m = (big[sums(c, 0, 1)] + big[R1 + c * 4 + 2]) + big[R2 + c * 2 + 1]
-        out[0, :, c * CW + HW:(c + 1) * CW] = (f[:, HW:] + m).astype(bf16)
+        xz[:, c * CW + HW:(c + 1) * CW] = (f[:, HW:] + m).astype(bf16)
+        result(c).start()
 
     barrier = pltpu.get_barrier_semaphore()
     for to in (px, py, pc):
         pl.semaphore_signal(barrier, inc=1, device_id=to, device_id_type=MESH)
+    loads = [pltpu.make_async_copy(src, dst, sem_in.at[i]) for i, (src, dst) in enumerate((
+        (h0_h, h0), (nm_h, nm), (na_h, na), (idx_h, idx), (slot_h, slot), (wr_h, wr), (cos_h, cos), (sin_h, sin),
+        (nf_h, nf)))]
+    for load in loads:
+        load.start()
     for i, src in enumerate((wk, wv)):
         pltpu.make_async_copy(src, ring.at[i, :, pl.ds(0, QT)], sem.at[i]).start()
+
+    for load in loads[:3]:
+        load.wait()
     for t in range(T_Q, NS):
-        start(t, T_Q, NS)
+        start(t)
 
     def norms(i, _):
         rows = pl.ds(pl.multiple_of(i * 16, 16), 16)
@@ -225,6 +243,8 @@
     for key in ('x0', 'y1', 'c0'):
         ag[key]().start()
 
+    for load in loads[3:]:
+        load.wait()
     logits = _dot(u[0, 0], wr[pl.ds(0, 512), :])
     for k in range(1, 4):
         logits = logits + _dot(u[0, k], wr[pl.ds(k * 512, 512), :])
@@ -253,8 +273,8 @@
     for n in range(4):
         kk[n] = rope(kf[:, n * HEAD:(n + 1) * HEAD])
         vv[n] = vf[:, n * HEAD:(n + 1) * HEAD].astype(bf16)
-    start(NS, T_Q, T_E2)
-    start(NS + 1, T_Q, T_E2)
+    start(NS)
+    start(NS + 1)
     causal = lax.broadcasted_iota(jnp.int32, (T, T), 0) >= lax.broadcasted_iota(jnp.int32, (T, T), 1)
 
     def q_dot(s, dst):
@@ -277,11 +297,11 @@
         t = T_Q + 2 * k + 1
         s = wait(t), wait(t + 1)
         q_dot(s[0], qb)
-        start(t + NS, T_EXP, T_E2)
         q_heads(2 * k, qa)
         q_dot(s[1], qa)
-        start(t + 1 + NS, T_EXP, T_E2)
         q_heads(2 * k + 1, qb)
+        start(t + NS, T_WO1, T_E2)
+        start(t + 1 + NS, T_WO1, T_E2)
 
         @pl.when(k == Q_FWD)
         def _():
@@ -297,17 +317,28 @@
         return 0
 
     q_dot(wait(T_Q), qa)
-    start(T_Q + NS, T_EXP, T_E2)
+    start(T_Q + NS)
     lax.fori_loop(0, NQ // 2 - 1, q_pair, 0)
-    s_last = wait(T_EXP - 1)
+    s_last = wait(T_WO1 - 1)
     q_dot(s_last, qb)
     q_heads(NQ - 2, qa)
     q_heads(NQ - 1, qb)
-    start(T_EXP - 1 + NS, T_EXP, T_E2)
+    start(T_WO1 - 1 + NS)
     for key in ('iy', 'id', 'x1', 'y0'):
         ag[key]().wait_recv()
     for key in ('icx', 'icy', 'icd', 'cx0', 'cy0'):
         ag[key]().start()
+
+    def wo_step(n, t):
+        cols = slice(n * CW, (n + 1) * CW)
+        s0, s1 = wait(t), wait(t + 1)
+        prod = _dot(g[:, :2048], ring[s0, :, pl.ds(0, CW)])
+        start(t + NS)
+        prod = prod + _dot(g[:, 2048:4096], ring[s1, :, pl.ds(0, CW)])
+        start(t + 1 + NS)
+        ar[:, cols] = (h0[0, :, cols].astype(f32) + prod).astype(bf16)
+
+    wo_step(0, T_WO1)
 
     base = ((ep * 32 + e0) * CAP).astype(f32)
 
@@ -345,6 +376,8 @@
     for key in ('d0', 'd1'):
         ag[key]().wait_recv()
     ag['cd0']().start()
+    for n in range(1, NW):
+        wo_step(n, T_WO1 + 2 * n)
     for key in ('icx', 'icy', 'icd', 'cx0', 'cy0'):
         ag[key]().wait_recv()
     lax.fori_loop(4, 7, build, 0)
@@ -457,16 +490,9 @@
     for c in range(NC):
         chunk(c)
 
-    for n in range(D // CW):
-        cols = slice(n * CW, (n + 1) * CW)
-        t = T_WO + 2 * n
-        s0, s1 = wait(t), wait(t + 1)
-        prod = _dot(g[:, :2048], ring[s0, :, pl.ds(0, CW)])
-        start(t + NS)
-        prod = prod + _dot(g[:, 2048:4096], ring[s1, :, pl.ds(0, CW)])
-        start(t + 1 + NS)
-        ar[:, cols] = (h0[0, :, cols].astype(f32) + prod).astype(bf16)
-        if n == 0:
+    for n in range(NW, NC):
+        wo_step(n, T_WO + 2 * (n - NW))
+        if n == NW:
             rs_first(NC - 1, (1, 2, 0))
             rs_second(1)
 
@@ -504,10 +530,12 @@
     for n in range(D // CW):
         cols = slice(n * CW, (n + 1) * CW)
         t = T_W2 + 3 * n
-        slots = [wait(t + k) for k in range(3)]
+        batch = n < NC - 1
+        slots = [wait(t + k) for k in range(3)] if batch else None
         prod = None
         for k in range(3):
-            term = _dot(g[:, k * 2048:(k + 1) * 2048], ring[slots[k], :, pl.ds(0, CW)])
+            s = slots[k] if batch else wait(t + k)
+            term = _dot(g[:, k * 2048:(k + 1) * 2048], ring[s, :, pl.ds(0, CW)])
             prod = term if prod is None else prod + term
             start(t + k + NS, T_W2, T_END)
         if n == 0:
@@ -522,6 +550,7 @@
     for c in range(NC):
         for name in ('c0', 'c1', 'c2', 'c3', 'xa', 'xb', 'ya', 'yb', 'y2', 'x2'):
             rs(name, c).wait_send()
+        result(c).wait()
 
 
 def solution(mesh):
@@ -534,14 +563,24 @@
     ncopies = 27 + 10 * NC
 
     def local(h0, idx, slot, na, wq, wk, wv, wo, nf, w1, w3, w2, nm, wr, ue1, ue3, ue2):
-        vm = pl.BlockSpec(memory_space=pltpu.VMEM)
         hb = pl.BlockSpec(memory_space=pl.ANY)
         return pl.pallas_call(
             _kernel,
             out_shape=jax.ShapeDtypeStruct(h0.shape, bf16),
-            in_specs=[vm] * 9 + [hb] * 10,
-            out_specs=vm,
+            in_specs=[hb] * 19,
+            out_specs=hb,
             scratch_shapes=[
+                pltpu.VMEM(h0.shape, bf16),
+                pltpu.VMEM((1, TOP, T), jnp.int32),
+                pltpu.VMEM((1, TOP, T), jnp.int32),
+                pltpu.VMEM((D,), bf16),
+                pltpu.VMEM((D,), bf16),
+                pltpu.VMEM((D,), bf16),
+                pltpu.VMEM((T, HEAD), f32),
+                pltpu.VMEM((T, HEAD), f32),
+                pltpu.VMEM(wr.shape, bf16),
+                pltpu.SemaphoreType.DMA((9,)),
+                pltpu.SemaphoreType.DMA((NC,)),
                 pltpu.VMEM((T, D), bf16),
                 pltpu.VMEM((T, D), bf16),
                 pltpu.VMEM((T, CW), f32),

time: 88.5 us -> 87 us (0.983)
  Pallas kernels: 86.5 us -> 84.9 us
    pallas_call x1, Pallas kernels: 86.5 us -> 84.9 us  [local(): pl.pallas_call(_kernel, out_shape=jax.ShapeDtypeStruct(h0.shape, bf16), i...]
where the time goes in v5:
time: 87 us; the launch traced here: 86.8 us
  Pallas kernels  84.9 us (98%)
  local copies, waits for them, and re-layouts  1.88 us (2%)
    pallas_call x1, Pallas kernels, local(): pl.pallas_call(_kernel, out_shape=jax.ShapeDtypeStruct(h0.shape, bf16), i...  84.9 us
    unnamed x1, local copies, waits for them, and re-layouts  1.88 us

profile of v5, /device:TPU:0, one launch (start us, length us, event | category | flops | bytes accessed | tf_op | source)
XLA Modules:
  0.0 86.8 jit_solution(9794210074949317792)
XLA Ops:
  0.0 84.9 %scmoe.1 = bf16[1,128,2048]{2,1,0:T(8,128)(2,1)} custom-call(bf16[1,128,2048]{2,1,0:T(8,128)(2,1)} %h0_h.1, s32[1,8,128]{2,1,0:T(8,128)} %bitcast.3, s32[1,8,128]{2,1,0:T(8,128)} %bitcast.4, bf16[2048]{0:T(1024)(128)(2,1)} %na_h.1, bf16[2048]{0:T(1024)(128)(2,1)} %nf_h.1, bf16[2048]{0:T(1024)(128)(2,1)} %nm_h.1, f32[128,128]{1,0:T(8,128)} %constant.4.clone.cos_h, ...), custom_call_target="tpu_custom_call" | custom-call | tf_op jit(solution)/shard_map/scmoe/pallas_call | solution.py:567
  84.9 1.9 %copy.21 = bf16[1,128,2048]{2,1,0:T(8,128)(2,1)} copy(bf16[1,128,2048]{2,1,0:T(8,128)(2,1)} %scmoe.1) | data formatting | bytes 1048576

commit v6 on v5

--- a/solution.py
+++ b/solution.py
@@ -54,7 +54,7 @@
 
 
 def _kernel(h0_h, idx_h, slot_h, na_h, nf_h, nm_h, cos_h, sin_h, wr_h, wq, wk, wv, wo, w1, w3, w2, ue1, ue3, ue2, out,
-            h0, idx, slot, na, nf, nm, cos, sin, wr, sem_in, sem_out, xz, ar, fs, qa, qb, u, info, ws, ds, x, kk, vv, g, big, ring,
+            h0, idx, slot, na, nf, nm, cos, sin, wr, sem_in, xz, ar, fs, qa, qb, u, info, ws, ds, x, kk, vv, g, big, ring,
             sem, send, recv, ready):
     dp, ep = lax.axis_index('dp'), lax.axis_index('ep')
     px = (dp, lax.rem(ep + 2, 4))
@@ -197,20 +197,15 @@
         big[sums(c, 1, 1)] = big[sums(c, 1, 1)] + big[R1 + c * 4 + 3]
         rs('x2', c).start()
 
-    def result(c):
-        cols = pl.ds(c * CW, CW)
-        return pltpu.make_async_copy(xz.at[:, cols], out.at[0, :, cols], sem_out.at[c])
-
     def rs_last(c, f):
         rs('xa', c).wait_recv()
         rs('y2', c).wait_recv()
         m = (big[sums(c, 0, 0)] + big[R1 + c * 4]) + big[R2 + c * 2]
-        xz[:, c * CW:c * CW + HW] = (f[:, :HW] + m).astype(bf16)
+        out[0, :, c * CW:c * CW + HW] = (f[:, :HW] + m).astype(bf16)
         rs('ya', c).wait_recv()
         rs('x2', c).wait_recv()
         m = (big[sums(c, 0, 1)] + big[R1 + c * 4 + 2]) + big[R2 + c * 2 + 1]
-        xz[:, c * CW + HW:(c + 1) * CW] = (f[:, HW:] + m).astype(bf16)
-        result(c).start()
+        out[0, :, c * CW + HW:(c + 1) * CW] = (f[:, HW:] + m).astype(bf16)
 
     barrier = pltpu.get_barrier_semaphore()
     for to in (px, py, pc):
@@ -550,7 +545,6 @@
     for c in range(NC):
         for name in ('c0', 'c1', 'c2', 'c3', 'xa', 'xb', 'ya', 'yb', 'y2', 'x2'):
             rs(name, c).wait_send()
-        result(c).wait()
 
 
 def solution(mesh):
@@ -566,9 +560,9 @@
         hb = pl.BlockSpec(memory_space=pl.ANY)
         return pl.pallas_call(
             _kernel,
-            out_shape=jax.ShapeDtypeStruct(h0.shape, bf16),
+            out_shape=pltpu.VMEM(h0.shape, bf16),
             in_specs=[hb] * 19,
-            out_specs=hb,
+            out_specs=pl.BlockSpec(memory_space=pltpu.VMEM),
             scratch_shapes=[
                 pltpu.VMEM(h0.shape, bf16),
                 pltpu.VMEM((1, TOP, T), jnp.int32),
@@ -580,7 +574,6 @@
                 pltpu.VMEM((T, HEAD), f32),
                 pltpu.VMEM(wr.shape, bf16),
                 pltpu.SemaphoreType.DMA((9,)),
-                pltpu.SemaphoreType.DMA((NC,)),
                 pltpu.VMEM((T, D), bf16),
                 pltpu.VMEM((T, D), bf16),
                 pltpu.VMEM((T, CW), f32),
@@ -602,7 +595,7 @@
                 pltpu.SemaphoreType.REGULAR,
             ],
             compiler_params=pltpu.CompilerParams(collective_id=0, has_side_effects=True,
-                                                 vmem_limit_bytes=67043328),
+                                                 vmem_limit_bytes=66100000),
             name='scmoe',
         )(h0, jnp.swapaxes(idx, 1, 2), jnp.swapaxes(slot, 1, 2), na, nf, nm,
           jnp.asarray(cos2), jnp.asarray(sin2), wr, wq, wk, wv, wo, w1, w3, w2, ue1, ue3, ue2.reshape(-1, D))

time: 87 us -> 85.2 us (0.979)
  local copies, waits for them, and re-layouts: 1.88 us -> 0.8 us
    unnamed x1, local copies, waits for them, and re-layouts: 1.88 us -> 0.8 us
where the time goes in v6:
time: 85.2 us; the launch traced here: 85.1 us
  Pallas kernels  84.3 us (99%)
    pallas_call x1, Pallas kernels, local(): pl.pallas_call(_kernel, out_shape=pltpu.VMEM(h0.shape, bf16), in_specs=[h...  84.3 us

profile of v6, /device:TPU:0, one launch (start us, length us, event | category | flops | bytes accessed | tf_op | source)
XLA Modules:
  0.0 85.1 jit_solution(16231930309535209018)
XLA Ops:
  0.0 84.3 %scmoe.1 = bf16[1,128,2048]{2,1,0:T(8,128)(2,1)S(1)} custom-call(bf16[1,128,2048]{2,1,0:T(8,128)(2,1)} %h0_h.1, s32[1,8,128]{2,1,0:T(8,128)} %bitcast.3, s32[1,8,128]{2,1,0:T(8,128)} %bitcast.4, bf16[2048]{0:T(1024)(128)(2,1)} %na_h.1, bf16[2048]{0:T(1024)(128)(2,1)} %nf_h.1, bf16[2048]{0:T(1024)(128)(2,1)} %nm_h.1, f32[128,128]{1,0:T(8,128)} %constant.4.clone.cos_h, ...), custom_call_target="tpu_custom_call" | custom-call | tf_op jit(solution)/shard_map/scmoe/pallas_call | solution.py:561
  84.3 0.8 copy.21

commit v7 on v6

--- a/solution.py
+++ b/solution.py
@@ -471,7 +471,9 @@
         if c == 2:
             rs_second(0)
 
-        for q in (7, 5, 6, 4, 3, 1, 2, 0):
+        for q in (7, 3, 5, 6, 4, 1, 2, 0):
+            if c == 0 and q == 2:
+                rs_first(c, (3,))
             r = PLACE[q]
             yr = x[:, r * CAP:(r + 1) * CAP, YC:YC + CW].reshape(2 * T, CW)
             three = _dot(ws[r], yr)
@@ -480,7 +482,8 @@
             big[sums(c, q, 1)] = m[:, HW:]
             if q >= 4:
                 rs('c%d' % (q - 4), c).start()
-        rs_first(c, (3,))
+        if c > 0:
+            rs_first(c, (3,))
 
     for c in range(NC):
         chunk(c)

time: 85.2 us -> 85 us (level)
  no operation moved by 1% of the time
where the time goes in v7:
time: 85 us; the launch traced here: 84.9 us
  Pallas kernels  84.1 us (99%)
    pallas_call x1, Pallas kernels, local(): pl.pallas_call(_kernel, out_shape=pltpu.VMEM(h0.shape, bf16), in_specs=[h...  84.1 us

profile of v7, /device:TPU:0, one launch (start us, length us, event | category | flops | bytes accessed | tf_op | source)
XLA Modules:
  0.0 84.9 jit_solution(15357520998857798517)
XLA Ops:
  0.0 84.1 %scmoe.1 = bf16[1,128,2048]{2,1,0:T(8,128)(2,1)S(1)} custom-call(bf16[1,128,2048]{2,1,0:T(8,128)(2,1)} %h0_h.1, s32[1,8,128]{2,1,0:T(8,128)} %bitcast.3, s32[1,8,128]{2,1,0:T(8,128)} %bitcast.4, bf16[2048]{0:T(1024)(128)(2,1)} %na_h.1, bf16[2048]{0:T(1024)(128)(2,1)} %nf_h.1, bf16[2048]{0:T(1024)(128)(2,1)} %nm_h.1, f32[128,128]{1,0:T(8,128)} %constant.4.clone.cos_h, ...), custom_call_target="tpu_custom_call" | custom-call | tf_op jit(solution)/shard_map/scmoe/pallas_call | solution.py:564
  84.1 0.8 copy.21
